TPU v7x, 32 devices: a 4x2x2 block of a 4x4x8 slice. The times are simulated.
32 devices in a mesh: dp: 4 (over y, z), tp: 8 (over x, core).
Axes of the slice: x: 4, y: 2, z: 2, core: 2. Of those that a mesh axis runs over, the one named last changes fastest.
The devices are a block of a 4x4x8 slice.
Arguments:
- out_y1: float32 [32, 128, 1024], P('dp'), parts along dimension 0
- out_y2: float32 [32, 128, 1024], P('dp'), parts along dimension 0
- cot_y1: float32 [32, 128, 1024], P('dp'), parts along dimension 0
- cot_y2: float32 [32, 128, 1024], P('dp'), parts along dimension 0
- w_qkv: bfloat16 [4, 1024, 8, 3, 128], P(None, None, 'tp')
- w_out: bfloat16 [4, 8, 128, 1024], P(None, 'tp')
- w_up: bfloat16 [4, 1024, 4096], P(None, None, 'tp')
- w_down: bfloat16 [4, 4096, 1024], P(None, 'tp')
Outputs:
- output 1: float32 [32, 128, 1024], P('dp'), parts along dimension 0
- output 2: float32 [32, 128, 1024], P('dp'), parts along dimension 0
- output 3: float32 [32, 128, 1024], P('dp'), parts along dimension 0
- output 4: float32 [32, 128, 1024], P('dp'), parts along dimension 0
- output 5: float32 [16, 1024, 8, 3, 128], P('dp', None, 'tp'), parts along dimension 0
- output 6: float32 [16, 8, 128, 1024], P('dp', 'tp'), parts along dimension 0
- output 7: float32 [16, 1024, 4096], P('dp', None, 'tp'), parts along dimension 0
- output 8: float32 [16, 4096, 1024], P('dp', 'tp'), parts along dimension 0
There are 4 independent parts. A program takes and returns all parts, laid end to end along the dimension named above; an argument that names none is the same for every part.
All inputs are finite; a program needn't handle non-finite values.
Results may differ from a plain program's by a relative error of at most 0.02.
Values are sent between devices in bfloat16 or wider.
A program may use at most 768 MiB of HBM per device.

v0:
```python
import math
import jax
import jax.numpy as jnp
from jax import lax
from jax.sharding import PartitionSpec as P

NORM_EPS = 1e-6


def rms_fwd(x_in):
    inv_rms = lax.rsqrt(jnp.mean(x_in * x_in, axis=-1, keepdims=True) + NORM_EPS)
    return inv_rms, x_in * inv_rms


def rms_back(norm_state, grad_n):
    inv_rms, normed = norm_state
    return inv_rms * (grad_n - normed * jnp.mean(normed * grad_n, axis=-1, keepdims=True))


def mlp_forward(x_in, w_up, w_down):
    norm_state = rms_fwd(x_in)
    n_bf = norm_state[1].astype(jnp.bfloat16)
    hidden = jnp.einsum("bsd,df->bsf", n_bf, w_up, preferred_element_type=jnp.float32)
    act_f, gelu_back = jax.vjp(jax.nn.gelu, hidden)
    act_bf = act_f.astype(jnp.bfloat16)
    part_sum = jnp.einsum("bsf,fd->bsd", act_bf, w_down, preferred_element_type=jnp.float32)
    return part_sum, norm_state, (n_bf, act_bf, gelu_back)


def mlp_backward(cot_out, w_up, w_down, saved):
    n_bf, act_bf, gelu_back = saved
    cot_bf = cot_out.astype(jnp.bfloat16)
    g_down = jnp.einsum("bsf,bsd->fd", act_bf, cot_bf, preferred_element_type=jnp.float32)
    grad_act = jnp.einsum("bsd,fd->bsf", cot_bf, w_down, preferred_element_type=jnp.float32)
    grad_hid = gelu_back(grad_act)[0].astype(jnp.bfloat16)
    g_up = jnp.einsum("bsd,bsf->df", n_bf, grad_hid, preferred_element_type=jnp.float32)
    grad_n = jnp.einsum("bsf,df->bsd", grad_hid, w_up, preferred_element_type=jnp.float32)
    return g_up, g_down, grad_n


def attn_forward(x_in, w_qkv, w_out):
    norm_state = rms_fwd(x_in)
    n_bf = norm_state[1].astype(jnp.bfloat16)
    score_scale = 1.0 / math.sqrt(w_qkv.shape[-1])
    qkv = jnp.einsum("bsd,dhje->bshje", n_bf, w_qkv, preferred_element_type=jnp.float32).astype(jnp.bfloat16)
    q_rows = qkv[:, :, :, 0]
    k_rows = qkv[:, :, :, 1]
    v_rows = qkv[:, :, :, 2]
    scores = jnp.einsum("bqhe,bkhe->bhqk", q_rows, k_rows, preferred_element_type=jnp.float32) * score_scale
    attn_prob = jax.nn.softmax(scores, axis=-1)
    prob_bf = attn_prob.astype(jnp.bfloat16)
    attn_out = jnp.einsum("bhqk,bkhe->bqhe", prob_bf, v_rows, preferred_element_type=jnp.float32).astype(jnp.bfloat16)
    part_sum = jnp.einsum("crif,ife->cre", attn_out, w_out, preferred_element_type=jnp.float32)
    return part_sum, norm_state, (n_bf, q_rows, k_rows, v_rows, attn_prob, prob_bf, attn_out)


def attn_backward(cot_out, w_qkv, w_out, saved):
    n_bf, q_rows, k_rows, v_rows, attn_prob, prob_bf, attn_out = saved
    score_scale = 1.0 / math.sqrt(w_qkv.shape[-1])
    cot_bf = cot_out.astype(jnp.bfloat16)
    g_out = jnp.einsum("crif,cre->ife", attn_out, cot_bf, preferred_element_type=jnp.float32)
    grad_o = jnp.einsum("cre,ife->crif", cot_bf, w_out, preferred_element_type=jnp.float32).astype(jnp.bfloat16)
    grad_p = jnp.einsum("bqhe,bkhe->bhqk", grad_o, v_rows, preferred_element_type=jnp.float32)
    grad_v = jnp.einsum("bhqk,bqhe->bkhe", prob_bf, grad_o, preferred_element_type=jnp.float32)
    grad_s = (attn_prob * (grad_p - jnp.sum(grad_p * attn_prob, axis=-1, keepdims=True)) * score_scale).astype(jnp.bfloat16)
    grad_q = jnp.einsum("bhqk,bkhe->bqhe", grad_s, k_rows, preferred_element_type=jnp.float32)
    grad_k = jnp.einsum("bhqk,bqhe->bkhe", grad_s, q_rows, preferred_element_type=jnp.float32)
    grad_qkv = jnp.stack([grad_q, grad_k, grad_v], axis=3).astype(jnp.bfloat16)
    g_qkv = jnp.einsum("bsd,bshje->dhje", n_bf, grad_qkv, preferred_element_type=jnp.float32)
    grad_n = jnp.einsum("bshje,dhje->bsd", grad_qkv, w_qkv, preferred_element_type=jnp.float32)
    return g_qkv, g_out, grad_n


def solution(mesh):
    act_spec = P("dp", None, None)
    weight_specs = (P(None, None, "tp", None, None), P(None, "tp", None, None), P(None, None, "tp"), P(None, "tp", None))
    grad_specs = (P("dp", None, "tp", None, None), P("dp", "tp", None, None), P("dp", None, "tp"), P("dp", "tp", None))

    def local_backward(out_y1, out_y2, cot_y1, cot_y2, w_qkv, w_out, w_up, w_down):
        run_y1, run_y2, run_c1, run_c2 = out_y1, out_y2, cot_y1, cot_y2
        per_layer = []
        for layer_idx in reversed(range(w_qkv.shape[0])):
            g_part, g_norm, g_saved = mlp_forward(run_y1, w_up[layer_idx], w_down[layer_idx])
            low_x2 = run_y2 - lax.psum(g_part, "tp")
            g_up, g_down, gn_part = mlp_backward(run_c2, w_up[layer_idx], w_down[layer_idx], g_saved)
            grad_n = lax.psum(gn_part.astype(jnp.bfloat16), "tp").astype(jnp.float32)
            run_c1 = run_c1 + rms_back(g_norm, grad_n)
            f_part, f_norm, f_saved = attn_forward(low_x2, w_qkv[layer_idx], w_out[layer_idx])
            run_y1 = run_y1 - lax.psum(f_part, "tp")
            g_qkv, g_out, fn_part = attn_backward(run_c1, w_qkv[layer_idx], w_out[layer_idx], f_saved)
            grad_n = lax.psum(fn_part.astype(jnp.bfloat16), "tp").astype(jnp.float32)
            run_c2 = run_c2 + rms_back(f_norm, grad_n)
            run_y2 = low_x2
            per_layer.append((g_qkv, g_out, g_up, g_down))
        per_layer = per_layer[::-1]
        stacked = [jnp.stack([layer_grads[slot_idx] for layer_grads in per_layer]) for slot_idx in range(4)]
        return (run_y1, run_y2, run_c1, run_c2, stacked[0], stacked[1], stacked[2], stacked[3])

    return jax.shard_map(local_backward, mesh=mesh, in_specs=(act_spec, act_spec, act_spec, act_spec) + weight_specs, out_specs=(act_spec, act_spec, act_spec, act_spec) + grad_specs, check_vma=False)
```

profile of v0, /device:TPU:81, one launch (start us, length us, event | category | flops | bytes accessed | tf_op | source)
XLA Modules:
  0.0 1183.2 jit_solution(9455621652434981309)
XLA Ops:
  13.2 5.4 fusion.171
  18.8 4.9 fusion.38
  24.6 3.8 convolution_convert_fusion.3
  28.6 58.5 %all-reduce.17.cloned.1.call-done = f32[8,128,1024]{2,1,0:T(8,128)} async-done(((f32[8,128,1024]{2,1,0:T(8,128)}), f32[8,128,1024]{2,1,0:T(8,128)}) %all-reduce.17.cloned.1.call-update) | async-done | bytes 4194320 | tf_op jit(solution)/shard_map/psum | solution.py:84
  87.1 4.0 multiply_reduce_fusion.6
  100.3 49.0 %all-reduce.33.cloned.1.call-done = bf16[8,128,1024]{2,1,0:T(8,128)(2,1)} async-done(((bf16[8,128,1024]{2,1,0:T(8,128)(2,1)}), bf16[8,128,1024]{2,1,0:T(8,128)(2,1)}) %all-reduce.33.cloned.1.call-update) | async-done | bytes 2097168 | tf_op jit(solution)/shard_map/psum | solution.py:86
  149.3 3.7 fusion.8
  153.0 64.9 %all-reduce.19.cloned.1.call-done = f32[8,128,1024]{2,1,0:T(8,128)} async-done(((f32[8,128,1024]{2,1,0:T(8,128)}), f32[8,128,1024]{2,1,0:T(8,128)}) %all-reduce.19.cloned.1.call-update) | async-done | bytes 4194320 | tf_op jit(solution)/shard_map/psum | solution.py:89
  217.9 6.9 multiply_reduce_fusion.5
  230.4 3.9 bitcast_convert_fusion.3
  234.5 3.8 fusion.168
  239.6 4.6 fusion.165
  244.4 49.4 %all-reduce.35.cloned.1.call-done = bf16[8,128,1024]{2,1,0:T(8,128)(2,1)} async-done(((bf16[8,128,1024]{2,1,0:T(8,128)(2,1)}), bf16[8,128,1024]{2,1,0:T(8,128)(2,1)}) %all-reduce.35.cloned.1.call-update) | async-done | bytes 2097168 | tf_op jit(solution)/shard_map/psum | solution.py:91
  293.8 3.7 fusion.11
  297.4 64.8 %all-reduce.21.cloned.1.call-done = f32[8,128,1024]{2,1,0:T(8,128)} async-done(((f32[8,128,1024]{2,1,0:T(8,128)}), f32[8,128,1024]{2,1,0:T(8,128)}) %all-reduce.21.cloned.1.call-update) | async-done | bytes 4194320 | tf_op jit(solution)/shard_map/psum | solution.py:84
  362.2 7.0 multiply_reduce_fusion.4
  369.3 4.4 fusion.45
  374.7 3.8 convolution_convert_fusion.2
  378.9 3.7 fusion.106
  386.1 51.8 %all-reduce.37.cloned.1.call-done = bf16[8,128,1024]{2,1,0:T(8,128)(2,1)} async-done(((bf16[8,128,1024]{2,1,0:T(8,128)(2,1)}), bf16[8,128,1024]{2,1,0:T(8,128)(2,1)}) %all-reduce.37.cloned.1.call-update) | async-done | bytes 2097168 | tf_op jit(solution)/shard_map/psum | solution.py:86
  438.0 3.7 fusion.14
  441.6 64.9 %all-reduce.23.cloned.1.call-done = f32[8,128,1024]{2,1,0:T(8,128)} async-done(((f32[8,128,1024]{2,1,0:T(8,128)}), f32[8,128,1024]{2,1,0:T(8,128)}) %all-reduce.23.cloned.1.call-update) | async-done | bytes 4194320 | tf_op jit(solution)/shard_map/psum | solution.py:89
  506.5 6.9 multiply_reduce_fusion.3
  518.9 3.9 bitcast_convert_fusion.2
  523.0 3.8 fusion.162
  528.1 4.6 fusion.159
  533.3 4.0 convolution_bitcast_fusion.4
  545.8 36.5 %all-reduce.39.cloned.1.call-done = bf16[8,128,1024]{2,1,0:T(8,128)(2,1)} async-done(((bf16[8,128,1024]{2,1,0:T(8,128)(2,1)}), bf16[8,128,1024]{2,1,0:T(8,128)(2,1)}) %all-reduce.39.cloned.1.call-update) | async-done | bytes 2097168 | tf_op jit(solution)/shard_map/psum | solution.py:91
  582.3 3.5 fusion.17
  585.8 65.0 %all-reduce.25.cloned.1.call-done = f32[8,128,1024]{2,1,0:T(8,128)} async-done(((f32[8,128,1024]{2,1,0:T(8,128)}), f32[8,128,1024]{2,1,0:T(8,128)}) %all-reduce.25.cloned.1.call-update) | async-done | bytes 4194320 | tf_op jit(solution)/shard_map/psum | solution.py:84
  650.9 8.1 multiply_reduce_fusion.2
  659.0 4.4 fusion.52
  664.4 3.8 convolution_convert_fusion.1
  668.4 4.6 fusion.103
  679.7 5.4 convolution_bitcast_fusion.5
  693.1 34.6 %all-reduce.41.cloned.1.call-done = bf16[8,128,1024]{2,1,0:T(8,128)(2,1)} async-done(((bf16[8,128,1024]{2,1,0:T(8,128)(2,1)}), bf16[8,128,1024]{2,1,0:T(8,128)(2,1)}) %all-reduce.41.cloned.1.call-update) | async-done | bytes 2097168 | tf_op jit(solution)/shard_map/psum | solution.py:86
  727.7 3.5 fusion.20
  731.2 65.0 %all-reduce.27.cloned.1.call-done = f32[8,128,1024]{2,1,0:T(8,128)} async-done(((f32[8,128,1024]{2,1,0:T(8,128)}), f32[8,128,1024]{2,1,0:T(8,128)}) %all-reduce.27.cloned.1.call-update) | async-done | bytes 4194320 | tf_op jit(solution)/shard_map/psum | solution.py:89
  796.3 8.0 multiply_reduce_fusion.1
  814.7 4.0 bitcast_convert_fusion.1
  818.8 3.8 fusion.156
  824.0 4.6 fusion.153
  829.0 5.4 convolution_bitcast_fusion.6
  839.6 2.8 fusion.82
  842.4 35.7 %all-reduce.43.cloned.1.call-done = bf16[8,128,1024]{2,1,0:T(8,128)(2,1)} async-done(((bf16[8,128,1024]{2,1,0:T(8,128)(2,1)}), bf16[8,128,1024]{2,1,0:T(8,128)(2,1)}) %all-reduce.43.cloned.1.call-update) | async-done | bytes 2097168 | tf_op jit(solution)/shard_map/psum | solution.py:91
  878.1 3.5 fusion.23
  881.7 65.0 %all-reduce.29.cloned.1.call-done = f32[8,128,1024]{2,1,0:T(8,128)} async-done(((f32[8,128,1024]{2,1,0:T(8,128)}), f32[8,128,1024]{2,1,0:T(8,128)}) %all-reduce.29.cloned.1.call-update) | async-done | bytes 4194320 | tf_op jit(solution)/shard_map/psum | solution.py:84
  946.7 8.1 multiply_reduce_fusion
  954.8 4.4 fusion.59
  960.2 3.8 convolution_convert_fusion
  964.2 4.6 fusion.100
  975.6 4.3 convolution_bitcast_fusion.3
  980.3 4.4 pad_maximum_fusion.1
  987.9 3.8 pad_maximum_fusion
  991.7 31.8 %all-reduce.45.cloned.1.call-done = bf16[8,128,1024]{2,1,0:T(8,128)(2,1)} async-done(((bf16[8,128,1024]{2,1,0:T(8,128)(2,1)}), bf16[8,128,1024]{2,1,0:T(8,128)(2,1)}) %all-reduce.45.cloned.1.call-update) | async-done | bytes 2097168 | tf_op jit(solution)/shard_map/psum | solution.py:86
  1023.5 3.7 fusion.26
  1027.2 64.7 %all-reduce.31.cloned.1.call-done = f32[8,128,1024]{2,1,0:T(8,128)} async-done(((f32[8,128,1024]{2,1,0:T(8,128)}), f32[8,128,1024]{2,1,0:T(8,128)}) %all-reduce.31.cloned.1.call-update) | async-done | bytes 4194320 | tf_op jit(solution)/shard_map/psum | solution.py:89
  1091.9 7.1 fusion.28
  1103.2 3.8 bitcast_convert_fusion
  1107.1 3.9 fusion.85
  1111.5 7.5 copy.72
  1122.0 44.4 %all-reduce.47.cloned.1.call-done = bf16[8,128,1024]{2,1,0:T(8,128)(2,1)} async-done(((bf16[8,128,1024]{2,1,0:T(8,128)(2,1)}), bf16[8,128,1024]{2,1,0:T(8,128)(2,1)}) %all-reduce.47.cloned.1.call-update) | async-done | bytes 2097168 | tf_op jit(solution)/shard_map/psum | solution.py:91
  1166.4 3.7 fusion.29
  1171.1 5.1 fusion.31
  (249 shorter events, 97.6 us)
Async XLA Ops:
  7.2 79.9 %all-reduce.17.cloned.1.call-start = ((), (), s32[]{:S(2)}) async-start(), calls=%async_computation | async-start | bytes 8388608 | tf_op jit(solution)/shard_map/psum | solution.py:84
  7.2 3.5 copy-start
  13.2 5.6 copy-start.29
  18.7 130.6 %all-reduce.33.cloned.1.call-start = ((), (), s32[]{:S(2)}) async-start(), calls=%async_computation.8 | async-start | bytes 4194304 | tf_op jit(solution)/shard_map/psum | solution.py:86
  28.5 189.4 %all-reduce.19.cloned.1.call-start = ((), (), s32[]{:S(2)}) async-start(), calls=%async_computation.1 | async-start | bytes 8388608 | tf_op jit(solution)/shard_map/psum | solution.py:89
  95.6 4.5 copy-start.49
  96.0 4.1 copy-start.62
  100.1 193.7 %all-reduce.35.cloned.1.call-start = ((), (), s32[]{:S(2)}) async-start(), calls=%async_computation.9 | async-start | bytes 4194304 | tf_op jit(solution)/shard_map/psum | solution.py:91
  149.3 68.6 %copy-start.22 = (bf16[8,128,1024]{2,1,0:T(8,128)(2,1)S(1)}, bf16[8,128,1024]{2,1,0:T(8,128)(2,1)}, u32[]{:S(2)}) copy-start(bf16[8,128,1024]{2,1,0:T(8,128)(2,1)} %all-reduce.33.cloned.1.call-done) | copy-start | bytes 6291460
  234.4 127.8 %all-reduce.21.cloned.1.call-start = ((), (), s32[]{:S(2)}) async-start(), calls=%async_computation.2 | async-start | bytes 8388608 | tf_op jit(solution)/shard_map/psum | solution.py:84
  244.3 193.6 %all-reduce.37.cloned.1.call-start = ((), (), s32[]{:S(2)}) async-start(), calls=%async_computation.10 | async-start | bytes 4194304 | tf_op jit(solution)/shard_map/psum | solution.py:86
  293.7 68.5 %copy-start.24 = (bf16[8,128,1024]{2,1,0:T(8,128)(2,1)S(1)}, bf16[8,128,1024]{2,1,0:T(8,128)(2,1)}, u32[]{:S(2)}) copy-start(bf16[8,128,1024]{2,1,0:T(8,128)(2,1)} %all-reduce.35.cloned.1.call-done) | copy-start | bytes 6291460
  362.2 7.1 copy-start.32
  369.2 4.4 copy-start.16
  378.6 127.9 %all-reduce.23.cloned.1.call-start = ((), (), s32[]{:S(2)}) async-start(), calls=%async_computation.3 | async-start | bytes 8388608 | tf_op jit(solution)/shard_map/psum | solution.py:89
  382.6 3.4 copy-start.51
  382.9 3.1 copy-start.64
  383.2 2.8 copy-start.58
  386.1 196.2 %all-reduce.39.cloned.1.call-start = ((), (), s32[]{:S(2)}) async-start(), calls=%async_computation.11 | async-start | bytes 4194304 | tf_op jit(solution)/shard_map/psum | solution.py:91
  437.9 68.6 %copy-start.23 = (bf16[8,128,1024]{2,1,0:T(8,128)(2,1)S(1)}, bf16[8,128,1024]{2,1,0:T(8,128)(2,1)}, u32[]{:S(2)}) copy-start(bf16[8,128,1024]{2,1,0:T(8,128)(2,1)} %all-reduce.37.cloned.1.call-done) | copy-start | bytes 6291460
  522.9 128.0 %all-reduce.25.cloned.1.call-start = ((), (), s32[]{:S(2)}) async-start(), calls=%async_computation.4 | async-start | bytes 8388608 | tf_op jit(solution)/shard_map/psum | solution.py:84
  532.8 194.9 %all-reduce.41.cloned.1.call-start = ((), (), s32[]{:S(2)}) async-start(), calls=%async_computation.12 | async-start | bytes 4194304 | tf_op jit(solution)/shard_map/psum | solution.py:86
  533.3 4.0 copy-start.28
  533.3 4.4 copy-start.30
  537.7 2.8 copy-start.7
  540.5 2.4 copy-start.67
  540.5 2.5 copy-start.68
  540.5 2.5 copy-start.69
  650.9 8.1 copy-start.35
  659.0 4.4 copy-start.18
  668.3 128.0 %all-reduce.27.cloned.1.call-start = ((), (), s32[]{:S(2)}) async-start(), calls=%async_computation.5 | async-start | bytes 8388608 | tf_op jit(solution)/shard_map/psum | solution.py:89
  679.4 198.7 %all-reduce.43.cloned.1.call-start = ((), (), s32[]{:S(2)}) async-start(), calls=%async_computation.13 | async-start | bytes 4194304 | tf_op jit(solution)/shard_map/psum | solution.py:91
  679.6 5.4 copy-start.17
  679.6 5.4 copy-start.33
  685.0 2.8 copy-start.9
  685.0 2.8 copy-start.59
  687.8 2.4 copy-start.5
  687.8 2.4 copy-start.71
  687.8 2.5 copy-start.72
  687.8 2.5 copy-start.73
  818.8 127.9 %all-reduce.29.cloned.1.call-start = ((), (), s32[]{:S(2)}) async-start(), calls=%async_computation.6 | async-start | bytes 8388608 | tf_op jit(solution)/shard_map/psum | solution.py:84
  828.7 194.8 %all-reduce.45.cloned.1.call-start = ((), (), s32[]{:S(2)}) async-start(), calls=%async_computation.14 | async-start | bytes 4194304 | tf_op jit(solution)/shard_map/psum | solution.py:86
  828.9 5.4 copy-start.19
  829.0 5.4 copy-start.36
  834.3 2.7 copy-start.11
  837.0 2.4 copy-start.74
  837.0 2.5 copy-start.75
  837.0 2.5 copy-start.76
  946.7 8.1 copy-start.38
  954.8 4.4 copy-start.15
  964.1 127.8 %all-reduce.31.cloned.1.call-start = ((), (), s32[]{:S(2)}) async-start(), calls=%async_computation.7 | async-start | bytes 8388608 | tf_op jit(solution)/shard_map/psum | solution.py:89
  975.2 191.1 %all-reduce.47.cloned.1.call-start = ((), (), s32[]{:S(2)}) async-start(), calls=%async_computation.15 | async-start | bytes 4194304 | tf_op jit(solution)/shard_map/psum | solution.py:91
  975.6 4.4 copy-start.42
  975.6 4.4 copy-start.43
  975.6 4.7 copy-start.44
  980.3 4.5 copy-start.1
  980.3 5.4 copy-start.57
  1023.5 68.4 %copy-start.26 = (bf16[8,128,1024]{2,1,0:T(8,128)(2,1)S(1)}, bf16[8,128,1024]{2,1,0:T(8,128)(2,1)}, u32[]{:S(2)}) copy-start(bf16[8,128,1024]{2,1,0:T(8,128)(2,1)} %all-reduce.45.cloned.1.call-done) | copy-start | bytes 6291460
  1107.0 3.9 copy-start.45
  1107.0 3.9 copy-start.46
  1107.1 3.9 copy-start.47
  1111.5 7.5 copy-start.14
  1166.4 4.0 copy-start.2
  1166.4 4.7 copy-start.25
  (29 other events, 47.4 us)
Sparse Core Ops, SparseCore 0:
  18.8 68.2 all-reduce.16
  90.1 59.1 all-reduce.32
  152.3 65.5 all-reduce.18
  234.5 59.1 all-reduce.34
  296.6 65.5 all-reduce.20
  378.7 59.1 all-reduce.36
  440.9 65.5 all-reduce.22
  523.0 59.2 all-reduce.38
  585.3 65.5 all-reduce.24
  668.4 59.1 all-reduce.40
  730.7 65.5 all-reduce.26
  818.9 59.1 all-reduce.42
  881.1 65.5 all-reduce.28
  964.3 59.1 all-reduce.44
  1026.3 65.5 all-reduce.30
  1107.2 59.1 all-reduce.46
where the time goes:
time: 1190 us; the launch traced here: 1180 us
  waiting for transfers between devices  847 us (71%)
  matrix products  182 us (15%)
  other arithmetic  103 us (9%)
  local copies, waits for them, and re-layouts  33.6 us (3%)
  between operations  15.2 us (1%)
    psum x4, waiting for transfers between devices, local_backward(): run_y1 = run_y1 - lax.psum(f_part, 'tp')  260 us
    psum x4, waiting for transfers between devices, local_backward(): low_x2 = run_y2 - lax.psum(g_part, 'tp')  253 us
    psum x4, waiting for transfers between devices, local_backward(): grad_n = lax.psum(gn_part.astype(jnp.bfloat16), 'tp').astype(jnp.float32)  167 us
    psum x4, waiting for transfers between devices, local_backward(): grad_n = lax.psum(fn_part.astype(jnp.bfloat16), 'tp').astype(jnp.float32)  166 us
    reduce_sum x8, other arithmetic, rms_fwd(): jnp.mean(x_in * x_in, axis=-1, keepdims=True) + NORM_EPS  51.7 us
    unnamed x155, local copies, waits for them, and re-layouts  33.6 us
    reduce_sum x8, other arithmetic, rms_back(): jnp.mean(normed * grad_n, axis=-1, keepdims=True)  29 us
  transfers between devices with their start and end apart: 16, of which 16 were waited for; matrix products, arithmetic and copies ran while one was open for 14% of the time, Pallas kernels for 0%

commit v1 on v0

v1 whole, which is shorter than its diff:
```python
import functools
import math
import jax
import jax.numpy as jnp
from jax import lax
from jax.experimental import pallas as pl
from jax.experimental.pallas import tpu as pltpu
from jax.sharding import PartitionSpec as P

NORM_EPS = 1e-6
F32, BF16 = jnp.float32, jnp.bfloat16
GELU_C = math.sqrt(2.0 / math.pi)
GELU_A = 0.044715
NCHIP = 4


def mm(a, b):
    return lax.dot_general(a, b, (((1,), (0,)), ((), ())), preferred_element_type=F32)


def mm_t(a, b):
    return lax.dot_general(a, b, (((1,), (1,)), ((), ())), preferred_element_type=F32)


def tmm(a, b):
    return lax.dot_general(a, b, (((0,), (0,)), ((), ())), preferred_element_type=F32)


def kernel(y1_hbm, y2_hbm, c1_hbm, c2_hbm, wqkv_hbm, wo_hbm, wu_hbm, wd_hbm,
           x1_out, x2_out, g1_out, g2_out, gqkv_out, gout_out, gup_out, gdown_out,
           N1, N2, D1, D2, Wqkv, Wo, Wu, Wd, Gqkv, Go, Gu, Gd, H, ACT, GH, QKV, PROB, O, GQ,
           Y1, Y2, C1, C2, PF, PB, XF, XB, RF, RB,
           ag_send, ag_recv, rs_send, rs_recv, fg_send, fg_recv, w_sem, g_sem, io_sem, own_sem):
    layers = wqkv_hbm.shape[0]
    rows = y1_hbm.shape[1]
    half = rows // 2
    width = y1_hbm.shape[2]
    head = wo_hbm.shape[1]
    scale = 1.0 / math.sqrt(head)
    ndev = 2 * NCHIP
    me = lax.axis_index("tp")
    c = me // 2
    k = lax.rem(me, 2)
    sib = me + 1 - 2 * k
    left = lax.rem(me + ndev - 2, ndev)
    right = lax.rem(me + 2, ndev)
    cl = lax.rem(c + NCHIP - 1, NCHIP)
    cr = lax.rem(c + 1, NCHIP)
    co = lax.rem(c + 2, NCHIP)
    mine = pl.ds(pl.multiple_of(k * rows, rows), rows)
    other = pl.ds(pl.multiple_of((1 - k) * rows, rows), rows)

    def my_half(h):
        return pl.ds(pl.multiple_of(k * rows + h * half, half), half)

    def order(j):
        off = (2 + j) * (1 - j // 2) + (3 - j) * (j // 2)
        return lax.rem(c + off, NCHIP)

    def remote(src, dst, ssem, rsem, dev):
        return pltpu.make_async_remote_copy(src_ref=src, dst_ref=dst, send_sem=ssem, recv_sem=rsem,
                                            device_id={"tp": dev}, device_id_type=pl.DeviceIdType.MESH)

    barrier = pltpu.get_barrier_semaphore()
    for dev in (sib, left, right):
        pl.semaphore_signal(barrier, inc=1, device_id={"tp": dev}, device_id_type=pl.DeviceIdType.MESH)
    pl.semaphore_wait(barrier, 3)

    class Gather:
        def __init__(self, view, ssem, rsem):
            def full(chip):
                return view(chip, mine)

            def sibrows(chip):
                return view(chip, other)

            def hf(chip, h):
                return view(chip, my_half(h))

            def ohf(chip, h):
                return view(chip, pl.ds(pl.multiple_of((1 - k) * rows + h * half, half), half))

            self.send = [
                remote(full(c), full(c), ssem.at[0], rsem.at[0], left),
                remote(full(c), full(c), ssem.at[1], rsem.at[1], right),
                remote(full(c), full(c), ssem.at[2], rsem.at[2], sib),
                remote(hf(cr, 0), hf(cr, 0), ssem.at[3], rsem.at[3], left),
                remote(full(cr), full(cr), ssem.at[4], rsem.at[4], sib),
                remote(hf(cl, 1), hf(cl, 1), ssem.at[5], rsem.at[5], right),
                remote(full(cl), full(cl), ssem.at[6], rsem.at[6], sib),
                remote(hf(co, 0), hf(co, 0), ssem.at[7], rsem.at[7], sib),
                remote(hf(co, 1), hf(co, 1), ssem.at[8], rsem.at[8], sib),
            ]
            land = [full(cr), full(cl), sibrows(c), hf(co, 0), sibrows(cr), hf(co, 1), sibrows(cl),
                    ohf(co, 0), ohf(co, 1)]
            self.recv = [remote(r, r, ssem.at[i], rsem.at[i], sib) for i, r in enumerate(land)]

        def start(self):
            for i in (0, 1, 2):
                self.send[i].start()

        def near(self):
            self.recv[0].wait_recv()
            self.send[3].start()
            self.send[4].start()
            self.recv[1].wait_recv()
            self.send[5].start()
            self.send[6].start()

        def far(self):
            self.recv[3].wait_recv()
            self.send[7].start()
            self.recv[5].wait_recv()
            self.send[8].start()

        def finish(self):
            for i in (2, 4, 6, 7, 8):
                self.recv[i].wait_recv()
            for cp in self.send:
                cp.wait_send()

    class Scatter:
        def __init__(self, part, from_sib, rec, ssem, rsem):
            self.part, self.from_sib = part, from_sib
            self.rel, self.dir, self.fin = rec.at[0], rec.at[1], rec.at[2]
            self.ssem, self.rsem = ssem, rsem

            def hp(chip, h):
                return part.at[chip, my_half(h)]

            def hr(buf, h):
                return buf.at[pl.ds(h * half, half)]

            def mk(i, src, dst, dev):
                return remote(src, dst, ssem.at[i], rsem.at[i], dev)

            self.opp = [mk(4, hp(co, 0), hr(self.rel, 0), left), mk(5, hp(co, 1), hr(self.rel, 1), right)]
            self.direct = [mk(6, hp(cl, 1), hr(self.dir, 1), left), mk(7, hp(cr, 0), hr(self.dir, 0), right)]
            self.relay = [mk(8, hp(cl, 0), hr(self.fin, 0), left), mk(9, hp(cr, 1), hr(self.fin, 1), right)]

        def pair(self, chip):
            return remote(self.part.at[chip, other], self.from_sib.at[chip], self.ssem.at[chip],
                          self.rsem.at[chip], sib)

        def add(self, chip):
            self.pair_recv(chip)
            got = self.part[chip, mine].astype(F32) + self.from_sib[chip].astype(F32)
            self.part[chip, mine] = got.astype(self.part.dtype)

        def pair_recv(self, chip):
            remote(self.from_sib.at[chip], self.from_sib.at[chip], self.ssem.at[chip], self.rsem.at[chip],
                   sib).wait_recv()

        def send_opp(self):
            self.add(co)
            for cp in self.opp:
                cp.start()

        def send_direct(self):
            self.add(cl)
            self.direct[0].start()
            self.add(cr)
            self.direct[1].start()

        def send_relay(self):
            for h, (chip, cp) in enumerate(((cl, self.relay[0]), (cr, self.relay[1]))):
                self.opp[h].wait_recv()
                got = self.part[chip, my_half(h)].astype(F32) + self.rel[h * half:(h + 1) * half].astype(F32)
                self.part[chip, my_half(h)] = got.astype(self.part.dtype)
                cp.start()

        def land(self):
            self.pair_recv(c)
            for cp in self.direct + self.relay:
                cp.wait_recv()

        def total(self, r):
            at = pl.ds(pl.multiple_of(k * rows + r * 16, 16), 16)
            loc = pl.ds(pl.multiple_of(r * 16, 16), 16)
            return (self.part[c, at].astype(F32) + self.from_sib[c, loc].astype(F32)
                    + self.fin[loc].astype(F32) + self.dir[loc].astype(F32))

        def drain(self):
            for chip in range(NCHIP):
                self.pair(chip).wait_send()
            for cp in self.opp + self.direct + self.relay:
                cp.wait_send()

    rs_f = Scatter(PF, XF, RF, rs_send.at[0], rs_recv.at[0])
    rs_b = Scatter(PB, XB, RB, rs_send.at[1], rs_recv.at[1])

    def gather_n(buf, par, i):
        return Gather(lambda chip, r: buf.at[par, chip, r], ag_send.at[i], ag_recv.at[i])

    def gather_d(buf, i):
        return Gather(lambda chip, r: buf.at[chip, r], ag_send.at[i], ag_recv.at[i])

    def gather_out(out, i):
        def view(chip, r):
            return out.at[pl.ds(pl.multiple_of(chip * 2 * rows, rows) + r.start, r.size)]
        return Gather(view, fg_send.at[i], fg_recv.at[i])

    def weight_copies(layer, slot):
        return [pltpu.make_async_copy(src.at[layer], dst.at[slot], w_sem.at[slot, i])
                for i, (src, dst) in enumerate(((wqkv_hbm, Wqkv), (wo_hbm, Wo), (wu_hbm, Wu), (wd_hbm, Wd)))]

    def grad_copy(layer, i):
        src, dst = ((Gqkv, gqkv_out), (Go, gout_out), (Gu, gup_out), (Gd, gdown_out))[i]
        return pltpu.make_async_copy(src, dst.at[layer], g_sem.at[i])

    def mlp_fwd(chip, par):
        hid = mm(N1[par, chip], Wu[par])
        H[chip] = hid
        act = hid * (0.5 * (1.0 + jnp.tanh(GELU_C * (hid + GELU_A * (hid * hid * hid)))))
        act = act.astype(BF16)
        ACT[chip] = act
        PF[chip] = mm(act, Wd[par])

    def mlp_bwd(chip, par):
        grad_act = mm_t(D2[chip], Wd[par])
        hid = H[chip]
        sq = hid * hid
        t = jnp.tanh(GELU_C * (hid + GELU_A * (sq * hid)))
        slope = 0.5 * (1.0 + t) + (0.5 * hid) * ((1.0 - t * t) * (GELU_C * (1.0 + (3.0 * GELU_A) * sq)))
        grad_hid = (grad_act * slope).astype(BF16)
        GH[chip] = grad_hid
        PB[chip] = mm_t(grad_hid, Wu[par]).astype(BF16)

    def attn_fwd(chip, par):
        QKV[chip] = mm(N2[par, chip], Wqkv[par]).astype(BF16)
        for s in range(2):
            at = slice(s * rows, (s + 1) * rows)
            q = QKV[chip, at, 0:head]
            kk = QKV[chip, at, head:2 * head]
            v = QKV[chip, at, 2 * head:3 * head]
            sc = mm_t(q, kk) * scale
            e = jnp.exp(sc - jnp.max(sc, axis=-1, keepdims=True))
            prob = e / jnp.sum(e, axis=-1, keepdims=True)
            PROB[chip, at] = prob
            O[chip, at] = mm(prob.astype(BF16), v).astype(BF16)
        PF[chip] = mm(O[chip], Wo[par])

    def attn_bwd(chip, par):
        grad_o2 = mm_t(D1[chip], Wo[par]).astype(BF16)
        for s in range(2):
            at = slice(s * rows, (s + 1) * rows)
            grad_o = grad_o2[at]
            q = QKV[chip, at, 0:head]
            kk = QKV[chip, at, head:2 * head]
            v = QKV[chip, at, 2 * head:3 * head]
            prob = PROB[chip, at]
            grad_p = mm_t(grad_o, v)
            grad_s = (prob * (grad_p - jnp.sum(grad_p * prob, axis=-1, keepdims=True)) * scale).astype(BF16)
            GQ[chip, at, 0:head] = mm(grad_s, kk).astype(BF16)
            GQ[chip, at, head:2 * head] = tmm(grad_s, q).astype(BF16)
            GQ[chip, at, 2 * head:3 * head] = tmm(prob.astype(BF16), grad_o).astype(BF16)
        PB[chip] = mm_t(GQ[chip], Wqkv[par]).astype(BF16)

    def flat(x):
        return x.reshape((x.shape[0] * x.shape[1],) + x.shape[2:])

    def mlp_wgrad(layer, par, not_first):
        @pl.when(not_first)
        def _():
            grad_copy(layer, 2).wait()
            grad_copy(layer, 3).wait()
        tile = width // 4

        def up(i, _):
            at = pl.ds(pl.multiple_of(i * tile, tile), tile)
            Gu[at] = tmm(flat(N1[par, :, :, at]), flat(GH[...]))
            return 0

        def down(i, _):
            at = pl.ds(pl.multiple_of(i * tile, tile), tile)
            Gd[:, at] = tmm(flat(ACT[...]), flat(D2[:, :, at]))
            return 0
        lax.fori_loop(0, 4, up, 0)
        grad_copy(layer, 2).start()
        lax.fori_loop(0, 4, down, 0)
        grad_copy(layer, 3).start()

    def attn_wgrad(layer, par, not_first):
        @pl.when(not_first)
        def _():
            grad_copy(layer, 0).wait()
            grad_copy(layer, 1).wait()
        tile = width // 4

        def qkv(i, _):
            at = pl.ds(pl.multiple_of(i * tile, tile), tile)
            Gqkv[at] = tmm(flat(N2[par, :, :, at]), flat(GQ[...]))
            return 0

        def out(i, _):
            at = pl.ds(pl.multiple_of(i * tile, tile), tile)
            Go[:, at] = tmm(flat(O[...]), flat(D1[:, :, at]))
            return 0
        lax.fori_loop(0, 4, qkv, 0)
        grad_copy(layer, 0).start()
        lax.fori_loop(0, 4, out, 0)
        grad_copy(layer, 1).start()

    def own_rows(step):
        def body(r, _):
            step(r, pl.ds(pl.multiple_of(r * 16, 16), 16), pl.ds(pl.multiple_of(k * rows + r * 16, 16), 16))
            return 0
        lax.fori_loop(0, rows // 16, body, 0)

    def inv_rms(x):
        return lax.rsqrt(jnp.mean(x * x, axis=-1, keepdims=True) + NORM_EPS)

    def finish_state(rs, old, new, norm_to):
        rs.land()

        def step(r, loc, at):
            x = old[loc] - rs.total(r)
            new[loc] = x
            if norm_to is not None:
                norm_to[c, at] = (x * inv_rms(x)).astype(BF16)
        own_rows(step)
        rs.drain()

    def finish_cot(rs, cot, x_ref, cast_to):
        rs.land()

        def step(r, loc, at):
            x = x_ref[loc]
            inv = inv_rms(x)
            normed = x * inv
            grad_n = rs.total(r)
            new = cot[loc] + inv * (grad_n - normed * jnp.mean(normed * grad_n, axis=-1, keepdims=True))
            cot[loc] = new
            if cast_to is not None:
                cast_to[c, at] = new.astype(BF16)
        own_rows(step)
        rs.drain()

    def when(cond, fn):
        if cond is True:
            fn()
        elif cond is not False:
            pl.when(cond)(fn)

    def partials(rs, compute, early):
        def body(j, _):
            chip = order(j)
            compute(chip)
            rs.pair(chip).start()
            if early:
                pl.when(j == 1)(rs.send_opp)
            return 0
        lax.fori_loop(0, NCHIP, body, 0)

    def half_step(ag_n, fin_n, ag_d, fin_d, fwd, bwd, wgrad, has_d):
        fin_n()
        ag_n.start()
        when(has_d, rs_b.send_relay)
        ag_n.near()

        def d_start():
            fin_d()
            ag_d.start()
        when(has_d, d_start)
        ag_n.far()
        ag_n.finish()
        partials(rs_f, fwd, True)
        when(has_d, ag_d.near)
        rs_f.send_direct()
        rs_f.send_relay()

        def d_end():
            ag_d.far()
            ag_d.finish()
        when(has_d, d_end)
        partials(rs_b, bwd, False)
        rs_b.send_opp()
        rs_b.send_direct()
        wgrad()

    def stage_attn(layer, par, not_first, last):
        q = 1 - par
        if not last:
            for cp in weight_copies(layer - 1, q):
                cp.start()
        half_step(
            gather_n(N2, par, 0), lambda: finish_state(rs_f, Y2.at[q], Y2.at[par], N2.at[par]),
            gather_d(D2, 1), lambda: finish_cot(rs_b, C2, Y2.at[q], D2),
            lambda chip: attn_fwd(chip, par), lambda chip: mlp_bwd(chip, par),
            lambda: mlp_wgrad(layer, par, not_first), not_first)

    def stage_mlp(layer, par, not_first):
        q = 1 - par

        def fin():
            finish_state(rs_f, Y1.at[par], Y1.at[q], N1.at[q])
            for cp in weight_copies(layer - 1, q):
                cp.wait()
        half_step(
            gather_n(N1, q, 2), fin,
            gather_d(D1, 3), lambda: finish_cot(rs_b, C1, Y1.at[par], D1),
            lambda chip: mlp_fwd(chip, q), lambda chip: attn_bwd(chip, par),
            lambda: attn_wgrad(layer, par, not_first), True)

    top = layers - 1
    tp = top % 2
    for cp in weight_copies(top, tp):
        cp.start()
    blk = pl.ds(pl.multiple_of(me * 1, 1), 1)
    loads = [pltpu.make_async_copy(src.at[me], dst, own_sem.at[i]) for i, (src, dst) in enumerate(
        ((y1_hbm, Y1.at[tp]), (y2_hbm, Y2.at[1 - tp]), (c1_hbm, C1), (c2_hbm, C2)))]
    for cp in loads:
        cp.start()

    def bulk(src, i, chip, s):
        return pltpu.make_async_copy(src.at[2 * chip + s], PF.at[chip, pl.ds(s * rows, rows)], io_sem.at[i, chip, s])

    for chip in range(NCHIP):
        for s in range(2):
            bulk(y1_hbm, 0, chip, s).start()
    for chip in range(NCHIP):
        for s in range(2):
            bulk(y1_hbm, 0, chip, s).wait()

    def norm_all(i, _):
        for chip in range(NCHIP):
            at = pl.ds(pl.multiple_of(i * 16, 16), 16)
            x = PF[chip, at]
            N1[tp, chip, at] = (x * inv_rms(x)).astype(BF16)
        return 0
    lax.fori_loop(0, 2 * rows // 16, norm_all, 0)
    for chip in range(NCHIP):
        for s in range(2):
            bulk(c2_hbm, 1, chip, s).start()
    for chip in range(NCHIP):
        for s in range(2):
            bulk(c2_hbm, 1, chip, s).wait()

    def cast_all(i, _):
        for chip in range(NCHIP):
            at = pl.ds(pl.multiple_of(i * 16, 16), 16)
            D2[chip, at] = PF[chip, at].astype(BF16)
        return 0
    lax.fori_loop(0, 2 * rows // 16, cast_all, 0)
    for cp in loads:
        cp.wait()
    for cp in weight_copies(top, tp):
        cp.wait()
    partials(rs_f, lambda chip: mlp_fwd(chip, tp), True)
    rs_f.send_direct()
    rs_f.send_relay()

    def layer_body(i, _):
        layer = top - i
        par = lax.rem(layer, 2)
        stage_attn(layer, par, layer < top, False)
        stage_mlp(layer, par, layer < top)
        return 0
    lax.fori_loop(0, top, layer_body, 0)

    stage_attn(0, 0, True, True)
    outs = [gather_out(o, i) for i, o in enumerate((x1_out, x2_out, g1_out, g2_out))]

    def put(i, src):
        out = (x1_out, x2_out, g1_out, g2_out)[i]
        at = pl.ds(pl.multiple_of(me * rows, rows), rows)
        pltpu.make_async_copy(src, out.at[at], own_sem.at[i]).start()
        for n, dev in enumerate((left, right, sib)):
            remote(src, out.at[at], fg_send.at[i, n], fg_recv.at[i, n], dev).start()

    def put_done(i, src):
        out = (x1_out, x2_out, g1_out, g2_out)[i]
        at = pl.ds(pl.multiple_of(me * rows, rows), rows)
        pltpu.make_async_copy(src, out.at[at], own_sem.at[i]).wait()

    ag_d1 = gather_d(D1, 3)
    finish_state(rs_f, Y1.at[0], Y1.at[1], None)
    rs_b.send_relay()
    put(1, Y2.at[0])
    finish_cot(rs_b, C1, Y1.at[0], D1)
    ag_d1.start()
    put(0, Y1.at[1])
    ag_d1.near()
    outs[1].near()
    ag_d1.far()
    ag_d1.finish()
    partials(rs_b, lambda chip: attn_bwd(chip, 0), False)
    rs_b.send_opp()
    rs_b.send_direct()
    put(2, C1)
    attn_wgrad(0, 0, True)
    outs[0].near()
    rs_b.send_relay()
    outs[1].far()
    finish_cot(rs_b, C2, Y2.at[0], None)
    put(3, C2)
    outs[0].far()
    outs[2].near()
    outs[3].near()
    outs[2].far()
    outs[3].far()
    for i, src in enumerate((Y1.at[1], Y2.at[0], C1, C2)):
        outs[i].finish()
        put_done(i, src)
    for i in range(4):
        grad_copy(0, i).wait()


def solution(mesh):
    act_spec = P("dp", None, None)
    weight_specs = (P(None, None, "tp", None, None), P(None, "tp", None, None), P(None, None, "tp"), P(None, "tp", None))
    grad_specs = (P("dp", None, "tp", None, None), P("dp", "tp", None, None), P("dp", None, "tp"), P("dp", "tp", None))

    def local_backward(out_y1, out_y2, cot_y1, cot_y2, w_qkv, w_out, w_up, w_down):
        seqs, rows, width = out_y1.shape
        layers, _, heads, three, head = w_qkv.shape
        hidden = w_up.shape[2]
        wq = w_qkv.reshape(layers, width, heads * three * head)
        wo = w_out.reshape(layers, heads * head, width)
        pair = 2 * rows
        qkv_w = three * head
        act = jax.ShapeDtypeStruct((seqs * rows, width), F32)
        dma = pltpu.SemaphoreType.DMA
        outs = pl.pallas_call(
            kernel,
            out_shape=(act, act, act, act,
                       jax.ShapeDtypeStruct((layers, width, qkv_w), F32),
                       jax.ShapeDtypeStruct((layers, head, width), F32),
                       jax.ShapeDtypeStruct((layers, width, hidden), F32),
                       jax.ShapeDtypeStruct((layers, hidden, width), F32)),
            in_specs=[pl.BlockSpec(memory_space=pl.ANY)] * 8,
            out_specs=[pl.BlockSpec(memory_space=pl.ANY)] * 8,
            scratch_shapes=[
                pltpu.VMEM((2, NCHIP, pair, width), BF16),
                pltpu.VMEM((2, NCHIP, pair, width), BF16),
                pltpu.VMEM((NCHIP, pair, width), BF16),
                pltpu.VMEM((NCHIP, pair, width), BF16),
                pltpu.VMEM((2, width, qkv_w), BF16),
                pltpu.VMEM((2, head, width), BF16),
                pltpu.VMEM((2, width, hidden), BF16),
                pltpu.VMEM((2, hidden, width), BF16),
                pltpu.VMEM((width, qkv_w), F32),
                pltpu.VMEM((head, width), F32),
                pltpu.VMEM((width, hidden), F32),
                pltpu.VMEM((hidden, width), F32),
                pltpu.VMEM((NCHIP, pair, hidden), F32),
                pltpu.VMEM((NCHIP, pair, hidden), BF16),
                pltpu.VMEM((NCHIP, pair, hidden), BF16),
                pltpu.VMEM((NCHIP, pair, qkv_w), BF16),
                pltpu.VMEM((NCHIP, pair, rows), F32),
                pltpu.VMEM((NCHIP, pair, head), BF16),
                pltpu.VMEM((NCHIP, pair, qkv_w), BF16),
                pltpu.VMEM((2, rows, width), F32),
                pltpu.VMEM((2, rows, width), F32),
                pltpu.VMEM((rows, width), F32),
                pltpu.VMEM((rows, width), F32),
                pltpu.VMEM((NCHIP, pair, width), F32),
                pltpu.VMEM((NCHIP, pair, width), BF16),
                pltpu.VMEM((NCHIP, rows, width), F32),
                pltpu.VMEM((NCHIP, rows, width), BF16),
                pltpu.VMEM((3, rows, width), F32),
                pltpu.VMEM((3, rows, width), BF16),
                dma((4, 9)), dma((4, 9)), dma((2, 10)), dma((2, 10)), dma((4, 9)), dma((4, 9)),
                dma((2, 4)), dma((4,)), dma((2, NCHIP, 2)), dma((4,)),
            ],
            compiler_params=pltpu.CompilerParams(collective_id=0, has_side_effects=True,
                                                 vmem_limit_bytes=60 * 1024 * 1024),
        )(out_y1, out_y2, cot_y1, cot_y2, wq, wo, w_up, w_down)
        x1, x2, g1, g2 = (o.reshape(seqs, rows, width) for o in outs[:4])
        return (x1, x2, g1, g2, outs[4].reshape(w_qkv.shape), outs[5].reshape(w_out.shape), outs[6], outs[7])

    return jax.shard_map(local_backward, mesh=mesh, in_specs=(act_spec, act_spec, act_spec, act_spec) + weight_specs, out_specs=(act_spec, act_spec, act_spec, act_spec) + grad_specs, check_vma=False)
```

time: 1190 us -> 490 us (0.41)
  waiting for transfers between devices: 847 us -> 0 us
  Pallas kernels: 0 us -> 434 us
  matrix products: 182 us -> 0 us
  other arithmetic: 103 us -> 0.01 us
  local copies, waits for them, and re-layouts: 33.6 us -> 54.9 us
  between operations: 15.2 us -> 0.66 us
    psum x16 -> x0, waiting for transfers between devices: 846 us -> none  [the longest x4 260 us: local_backward(): run_y1 = run_y1 - lax.psum(f_part, 'tp')]
    pallas_call x0 -> x1, Pallas kernels: none -> 434 us  [local_backward(): pl.pallas_call(kernel, out_shape=(act, act, act, act, jax.ShapeDtypeStruc...]
    dot_general x68 -> x0, matrix products: 177 us -> none  [the longest x4 19.3 us: mlp_forward(): jnp.einsum('bsf,fd->bsd', act_bf, w_down, preferred_element_type=jnp.floa...]
    reduce_sum x16 -> x0, other arithmetic: 80.7 us -> none  [the longest x8 51.7 us: rms_fwd(): jnp.mean(x_in * x_in, axis=-1, keepdims=True) + NORM_EPS]
    add x2 -> x0, other arithmetic: 12.2 us -> none  [the longest x1 7.1 us: local_backward(): run_c1 = run_c1 + rms_back(g_norm, grad_n)]
    unnamed x155 -> x25, local copies, waits for them, and re-layouts: 33.6 us -> 45.6 us
  transfers between devices with their start and end apart: 16 -> 0, of which waited for: 16 -> 0; matrix products, arithmetic and copies ran while one was open for 14% -> 0% of each run, Pallas kernels for 0% -> 0%
where the time goes in v1:
time: 490 us; the launch traced here: 489 us
  Pallas kernels  434 us (89%)
  local copies, waits for them, and re-layouts  54.9 us (11%)
    pallas_call x1, Pallas kernels, local_backward(): pl.pallas_call(kernel, out_shape=(act, act, act, act, jax.ShapeDtypeStruc...  434 us
    unnamed x25, local copies, waits for them, and re-layouts  45.6 us

profile of v1, /device:TPU:81, one launch (start us, length us, event | category | flops | bytes accessed | tf_op | source)
XLA Modules:
  0.0 489.1 jit_solution(16874310251473868403)
XLA Ops:
  0.6 3.2 copy.19
  3.8 2.8 copy.20.wqkv_hbm
  6.6 433.5 %shard_map.143 = (f32[1024,1024]{1,0:T(8,128)}, f32[1024,1024]{1,0:T(8,128)}, f32[1024,1024]{1,0:T(8,128)}, f32[1024,1024]{1,0:T(8,128)}, f32[4,1024,384]{2,1,0:...) custom-call(f32[8,128,1024]{2,1,0:T(8,128)} %y1_hbm.1, ...), custom_call_target="tpu_custom_call" | custom-call | tf_op jit(solution)/shard_map/pallas_call | solution.py:524
  440.1 6.6 %copy.21 = f32[4,1024,384]{1,2,0:T(8,128)} copy(f32[4,1024,384]{2,1,0:T(8,128)} %get-tuple-element.20) | data formatting | bytes 12582912 | tf_op jit(solution)/shard_map/pallas_call | solution.py:524
  446.7 15.7 %copy.22 = f32[4,1024,1,3,128]{4,2,3,1,0:T(1,128)} copy(f32[4,1024,1,3,128]{1,4,3,0,2:T(8,128)} %bitcast.10) | data formatting | bytes 12582912
  462.4 0.0 copy-start.2
  462.4 4.9 %copy.31 = f32[8,128,1024]{2,1,0:T(8,128)} copy(f32[8,128,1024]{2,1,0:T(8,128)} %bitcast.19) | data formatting | bytes 8388608
  467.3 0.0 copy-done.2
  467.3 0.0 copy-start.1
  467.3 2.1 copy.32
  469.5 1.6 copy-done.1
  471.0 0.0 copy-start
  471.0 0.0 slice-start.2
  471.0 2.1 copy.33
  473.2 1.6 copy-done
  474.7 0.0 copy-start.3
  474.7 0.0 slice-start.3
  474.7 2.1 copy.34
  476.9 1.2 copy-done.3
  478.1 0.0 slice-start
  478.1 1.3 copy.35
  479.4 0.0 slice-done.2
  479.4 0.7 slice-done.3
  480.1 0.0 slice-start.1
  480.1 4.3 copy.36
  484.3 0.0 slice-done
  484.3 1.4 slice-done.1
  485.7 3.4 copy.37
  (2 shorter events, 0.0 us)
Async XLA Ops:
  462.4 4.9 %copy-start.2 = (f32[1024,1024]{1,0:T(8,128)S(1)}, f32[1024,1024]{1,0:T(8,128)}, u32[]{:S(2)}) copy-start(f32[1024,1024]{1,0:T(8,128)} %get-tuple-element.17) | copy-start | bytes 12582916
  467.3 3.7 copy-start.1
  471.0 3.7 copy-start
  471.0 8.4 %slice-start.2 = ((s8[8388608]{0:T(1024)(128)(4,1)}), s8[4194304]{0:T(1024)(128)(4,1)S(1)}, s32[]{:S(2)}) async-start(s8[8388608]{0:T(1024)(128)(4,1)} %bitcast.14), calls=%async_computation.2 | async-start | bytes 8388608
  474.7 3.4 copy-start.3
  474.7 5.3 %slice-start.3 = ((s8[8388608]{0:T(1024)(128)(4,1)}), s8[4194304]{0:T(1024)(128)(4,1)S(1)}, s32[]{:S(2)}) async-start(s8[8388608]{0:T(1024)(128)(4,1)} %bitcast.14), calls=%async_computation.3 | async-start | bytes 8388608
  478.1 6.2 %slice-start = ((s8[8388608]{0:T(1024)(128)(4,1)}), s8[4194304]{0:T(1024)(128)(4,1)S(1)}, s32[]{:S(2)}) async-start(s8[8388608]{0:T(1024)(128)(4,1)} %bitcast.12), calls=%async_computation | async-start | bytes 8388608
  480.1 5.6 %slice-start.1 = ((s8[8388608]{0:T(1024)(128)(4,1)}), s8[4194304]{0:T(1024)(128)(4,1)S(1)}, s32[]{:S(2)}) async-start(s8[8388608]{0:T(1024)(128)(4,1)} %bitcast.12), calls=%async_computation.1 | async-start | bytes 8388608

commit v2 on v1

--- a/solution.py
+++ b/solution.py
@@ -201,11 +201,15 @@
         return Gather(view, fg_send.at[i], fg_recv.at[i])
 
     def weight_copies(layer, slot):
-        return [pltpu.make_async_copy(src.at[layer], dst.at[slot], w_sem.at[slot, i])
-                for i, (src, dst) in enumerate(((wqkv_hbm, Wqkv), (wo_hbm, Wo), (wu_hbm, Wu), (wd_hbm, Wd)))]
+        pairs = [(src.at[layer], dst.at[slot]) for src, dst in ((wo_hbm, Wo), (wu_hbm, Wu), (wd_hbm, Wd))]
+        pairs += [(wqkv_hbm.at[layer, j], Wqkv.at[slot, :, pl.ds(j * head, head)]) for j in range(3)]
+        return [pltpu.make_async_copy(src, dst, w_sem.at[slot, i]) for i, (src, dst) in enumerate(pairs)]
 
     def grad_copy(layer, i):
         src, dst = ((Gqkv, gqkv_out), (Go, gout_out), (Gu, gup_out), (Gd, gdown_out))[i]
+        if i == 0:
+            size = src.shape[0]
+            return pltpu.make_async_copy(src, dst.at[pl.ds(pl.multiple_of(layer * size, size), size)], g_sem.at[i])
         return pltpu.make_async_copy(src, dst.at[layer], g_sem.at[i])
 
     def mlp_fwd(chip, par):
@@ -289,7 +293,9 @@
 
         def qkv(i, _):
             at = pl.ds(pl.multiple_of(i * tile, tile), tile)
-            Gqkv[at] = tmm(flat(N2[par, :, :, at]), flat(GQ[...]))
+            res = tmm(flat(N2[par, :, :, at]), flat(GQ[...]))
+            for j in range(3):
+                Gqkv[pl.ds(i * (3 * tile) + j, tile, stride=3), :] = res[:, j * head:(j + 1) * head]
             return 0
 
         def out(i, _):
@@ -406,49 +412,63 @@
     tp = top % 2
     for cp in weight_copies(top, tp):
         cp.start()
-    blk = pl.ds(pl.multiple_of(me * 1, 1), 1)
     loads = [pltpu.make_async_copy(src.at[me], dst, own_sem.at[i]) for i, (src, dst) in enumerate(
         ((y1_hbm, Y1.at[tp]), (y2_hbm, Y2.at[1 - tp]), (c1_hbm, C1), (c2_hbm, C2)))]
     for cp in loads:
         cp.start()
 
-    def bulk(src, i, chip, s):
-        return pltpu.make_async_copy(src.at[2 * chip + s], PF.at[chip, pl.ds(s * rows, rows)], io_sem.at[i, chip, s])
-
-    for chip in range(NCHIP):
+    def load_y1(chip, s):
+        return pltpu.make_async_copy(y1_hbm.at[2 * chip + s], PF.at[chip, pl.ds(s * rows, rows)], io_sem.at[0, chip, s])
+
+    batch = Gd.shape[0] // rows
+
+    def load_c2(b, i):
+        return pltpu.make_async_copy(c2_hbm.at[b * batch + i], Gd.at[pl.ds(i * rows, rows)],
+                                     io_sem.at[1, i // 2, i % 2])
+
+    def top_fwd(chip):
         for s in range(2):
-            bulk(y1_hbm, 0, chip, s).start()
-    for chip in range(NCHIP):
-        for s in range(2):
-            bulk(y1_hbm, 0, chip, s).wait()
-
-    def norm_all(i, _):
-        for chip in range(NCHIP):
+            load_y1(chip, s).wait()
+
+        def norm(i, _):
             at = pl.ds(pl.multiple_of(i * 16, 16), 16)
             x = PF[chip, at]
             N1[tp, chip, at] = (x * inv_rms(x)).astype(BF16)
+            return 0
+        lax.fori_loop(0, 2 * rows // 16, norm, 0)
+        mlp_fwd(chip, tp)
+
+    def cast_c2(b):
+        for i in range(batch):
+            load_c2(b, i).wait()
+
+        def cast(i, _):
+            for n in range(batch // 2):
+                at = pl.ds(pl.multiple_of(i * 16, 16), 16)
+                D2[b * (batch // 2) + n, at] = Gd[pl.ds(pl.multiple_of(n * 2 * rows + i * 16, 16), 16)].astype(BF16)
+            return 0
+        lax.fori_loop(0, 2 * rows // 16, cast, 0)
+        if b + 1 < 2 * NCHIP // batch:
+            for i in range(batch):
+                load_c2(b + 1, i).start()
+
+    def start_y1(j, _):
+        for s in range(2):
+            load_y1(order(j), s).start()
         return 0
-    lax.fori_loop(0, 2 * rows // 16, norm_all, 0)
-    for chip in range(NCHIP):
-        for s in range(2):
-            bulk(c2_hbm, 1, chip, s).start()
-    for chip in range(NCHIP):
-        for s in range(2):
-            bulk(c2_hbm, 1, chip, s).wait()
-
-    def cast_all(i, _):
-        for chip in range(NCHIP):
-            at = pl.ds(pl.multiple_of(i * 16, 16), 16)
-            D2[chip, at] = PF[chip, at].astype(BF16)
-        return 0
-    lax.fori_loop(0, 2 * rows // 16, cast_all, 0)
+    lax.fori_loop(0, NCHIP, start_y1, 0)
+    for i in range(batch):
+        load_c2(0, i).start()
+    for cp in weight_copies(top, tp):
+        cp.wait()
+    partials(rs_f, top_fwd, True)
+    rs_f.send_direct()
+    cast_c2(0)
+    rs_f.send_relay()
+    for b in range(1, 2 * NCHIP // batch):
+        cast_c2(b)
     for cp in loads:
         cp.wait()
-    for cp in weight_copies(top, tp):
-        cp.wait()
-    partials(rs_f, lambda chip: mlp_fwd(chip, tp), True)
-    rs_f.send_direct()
-    rs_f.send_relay()
 
     def layer_body(i, _):
         layer = top - i
@@ -515,7 +535,7 @@
         seqs, rows, width = out_y1.shape
         layers, _, heads, three, head = w_qkv.shape
         hidden = w_up.shape[2]
-        wq = w_qkv.reshape(layers, width, heads * three * head)
+        wq = jnp.transpose(w_qkv.reshape(layers, width, three, head), (0, 2, 1, 3))
         wo = w_out.reshape(layers, heads * head, width)
         pair = 2 * rows
         qkv_w = three * head
@@ -524,7 +544,7 @@
         outs = pl.pallas_call(
             kernel,
             out_shape=(act, act, act, act,
-                       jax.ShapeDtypeStruct((layers, width, qkv_w), F32),
+                       jax.ShapeDtypeStruct((layers * width * three, head), F32),
                        jax.ShapeDtypeStruct((layers, head, width), F32),
                        jax.ShapeDtypeStruct((layers, width, hidden), F32),
                        jax.ShapeDtypeStruct((layers, hidden, width), F32)),
@@ -539,7 +559,7 @@
                 pltpu.VMEM((2, head, width), BF16),
                 pltpu.VMEM((2, width, hidden), BF16),
                 pltpu.VMEM((2, hidden, width), BF16),
-                pltpu.VMEM((width, qkv_w), F32),
+                pltpu.VMEM((width * three, head), F32),
                 pltpu.VMEM((head, width), F32),
                 pltpu.VMEM((width, hidden), F32),
                 pltpu.VMEM((hidden, width), F32),
@@ -561,7 +581,7 @@
                 pltpu.VMEM((3, rows, width), F32),
                 pltpu.VMEM((3, rows, width), BF16),
                 dma((4, 9)), dma((4, 9)), dma((2, 10)), dma((2, 10)), dma((4, 9)), dma((4, 9)),
-                dma((2, 4)), dma((4,)), dma((2, NCHIP, 2)), dma((4,)),
+                dma((2, 6)), dma((4,)), dma((2, NCHIP, 2)), dma((4,)),
             ],
             compiler_params=pltpu.CompilerParams(collective_id=0, has_side_effects=True,
                                                  vmem_limit_bytes=60 * 1024 * 1024),

time: 490 us -> 461 us (0.941)
  local copies, waits for them, and re-layouts: 54.9 us -> 30.1 us
    unnamed x25 -> x28, local copies, waits for them, and re-layouts: 45.6 us -> 30.1 us
    pallas_call x1 -> x0, local copies, waits for them, and re-layouts: 6.56 us -> none  [local_backward(): pl.pallas_call(kernel, out_shape=(act, act, act, act, jax.ShapeDtypeStruc...]
where the time goes in v2:
time: 461 us
  Pallas kernels  430 us (93%)
  local copies, waits for them, and re-layouts  30.1 us (7%)
    pallas_call x1, Pallas kernels, local_backward(): pl.pallas_call(kernel, out_shape=(act, act, act, act, jax.ShapeDtypeStruc...  430 us
    unnamed x28, local copies, waits for them, and re-layouts  30.1 us

profile of v2, /device:TPU:81, one launch (start us, length us, event | category | flops | bytes accessed | tf_op | source)
XLA Modules:
  0.0 461.0 jit_solution(2400525671528416686)
XLA Ops:
  0.6 430.2 %shard_map.143 = (f32[1024,1024]{1,0:T(8,128)}, f32[1024,1024]{1,0:T(8,128)}, f32[1024,1024]{1,0:T(8,128)}, f32[1024,1024]{1,0:T(8,128)}, f32[12288,128]{1,0:T(8...) custom-call(f32[8,128,1024]{2,1,0:T(8,128)} %y1_hbm.1, f32[8,128,1024]{2,1,0:T(8,128)} %y2_hbm.1, ...), custom_call_target="tpu_custom_call" | custom-call | tf_op jit(solution)/shard_map/pallas_call | solution.py:544
  430.8 0.0 copy-start.2
  430.8 4.9 %copy.28 = f32[8,128,1024]{2,1,0:T(8,128)} copy(f32[8,128,1024]{2,1,0:T(8,128)} %bitcast.22) | data formatting | bytes 8388608
  435.8 0.0 copy-done.2
  435.8 0.0 copy-start.1
  435.8 0.0 slice-start.4
  435.8 2.1 copy.29
  437.9 1.6 copy-done.1
  439.5 0.0 copy-start
  439.5 0.0 slice-start.5
  439.5 2.1 copy.30
  441.6 1.8 copy-done
  443.4 0.0 slice-start.2
  443.5 2.1 copy.31
  445.6 0.0 slice-done.4
  445.6 0.0 slice-done.5
  445.6 0.0 copy-start.3
  445.6 0.0 slice-start.3
  445.6 3.2 copy.32
  448.8 1.2 copy-done.3
  450.0 0.0 slice-start
  450.0 1.3 copy.33
  451.4 0.0 slice-done.2
  451.4 0.5 slice-done.3
  451.9 0.0 slice-start.1
  451.9 4.3 copy.34
  456.2 0.0 slice-done
  456.2 1.4 slice-done.1
  457.6 3.4 copy.35
  (3 shorter events, 0.0 us)
Async XLA Ops:
  430.8 5.0 %copy-start.2 = (f32[1024,1024]{1,0:T(8,128)S(1)}, f32[1024,1024]{1,0:T(8,128)}, u32[]{:S(2)}) copy-start(f32[1024,1024]{1,0:T(8,128)} %get-tuple-element.17) | copy-start | bytes 12582916
  435.8 3.7 copy-start.1
  435.8 9.8 %slice-start.4 = ((s8[6291456]{0:T(1024)(128)(4,1)}), s8[4194304]{0:T(1024)(128)(4,1)S(1)}, s32[]{:S(2)}) async-start(s8[6291456]{0:T(1024)(128)(4,1)} %bitcast.16), calls=%async_computation.4 | async-start | bytes 8388608
  439.5 4.0 copy-start
  439.5 6.1 %slice-start.5 = ((s8[6291456]{0:T(1024)(128)(4,1)}), s8[2097152]{0:T(1024)(128)(4,1)S(1)}, s32[]{:S(2)}) async-start(s8[6291456]{0:T(1024)(128)(4,1)} %bitcast.16), calls=%async_computation.5 | async-start | bytes 4194304
  443.4 7.9 %slice-start.2 = ((s8[8388608]{0:T(1024)(128)(4,1)}), s8[4194304]{0:T(1024)(128)(4,1)S(1)}, s32[]{:S(2)}) async-start(s8[8388608]{0:T(1024)(128)(4,1)} %bitcast.14), calls=%async_computation.2 | async-start | bytes 8388608
  445.6 4.4 copy-start.3
  445.6 6.3 %slice-start.3 = ((s8[8388608]{0:T(1024)(128)(4,1)}), s8[4194304]{0:T(1024)(128)(4,1)S(1)}, s32[]{:S(2)}) async-start(s8[8388608]{0:T(1024)(128)(4,1)} %bitcast.14), calls=%async_computation.3 | async-start | bytes 8388608
  450.0 6.1 %slice-start = ((s8[8388608]{0:T(1024)(128)(4,1)}), s8[4194304]{0:T(1024)(128)(4,1)S(1)}, s32[]{:S(2)}) async-start(s8[8388608]{0:T(1024)(128)(4,1)} %bitcast.12), calls=%async_computation | async-start | bytes 8388608
  451.9 5.7 %slice-start.1 = ((s8[8388608]{0:T(1024)(128)(4,1)}), s8[4194304]{0:T(1024)(128)(4,1)S(1)}, s32[]{:S(2)}) async-start(s8[8388608]{0:T(1024)(128)(4,1)} %bitcast.12), calls=%async_computation.1 | async-start | bytes 8388608

commit v3 on v2

--- a/solution.py
+++ b/solution.py
@@ -26,11 +26,12 @@
     return lax.dot_general(a, b, (((0,), (0,)), ((), ())), preferred_element_type=F32)
 
 
-def kernel(y1_hbm, y2_hbm, c1_hbm, c2_hbm, wqkv_hbm, wo_hbm, wu_hbm, wd_hbm,
-           x1_out, x2_out, g1_out, g2_out, gqkv_out, gout_out, gup_out, gdown_out,
+def kernel(groups, y1_hbm, y2_hbm, c1_hbm, c2_hbm, wqkv_hbm, wo_hbm, wu_hbm, wd_hbm,
+           x1_out, x2_out, g1_out, g2_out, gqkv_out, gout_out, gup_out, gdown_out, wof_hbm,
            N1, N2, D1, D2, Wqkv, Wo, Wu, Wd, Gqkv, Go, Gu, Gd, H, ACT, GH, QKV, PROB, O, GQ,
-           Y1, Y2, C1, C2, PF, PB, XF, XB, RF, RB,
-           ag_send, ag_recv, rs_send, rs_recv, fg_send, fg_recv, w_sem, g_sem, io_sem, own_sem):
+           Y1, Y2, C1, C2, PF, PB, XF, XB, RF, RB, VG, WoV, OF, FT,
+           ag_send, ag_recv, rs_send, rs_recv, fg_send, fg_recv, w_sem, g_sem, io_sem, own_sem,
+           wg_send, wg_recv, wx_send, wx_recv, wl_sem, o_send, o_recv):
     layers = wqkv_hbm.shape[0]
     rows = y1_hbm.shape[1]
     half = rows // 2
@@ -61,24 +62,32 @@
         return pltpu.make_async_remote_copy(src_ref=src, dst_ref=dst, send_sem=ssem, recv_sem=rsem,
                                             device_id={"tp": dev}, device_id_type=pl.DeviceIdType.MESH)
 
+    grp = lax.axis_index("dp")
     barrier = pltpu.get_barrier_semaphore()
-    for dev in (sib, left, right):
-        pl.semaphore_signal(barrier, inc=1, device_id={"tp": dev}, device_id_type=pl.DeviceIdType.MESH)
-    pl.semaphore_wait(barrier, 3)
+
+    def hello(axis, at, n):
+        def one(i, _):
+            pl.semaphore_signal(barrier, inc=1, device_id={axis: lax.rem(at + i, n)},
+                                device_id_type=pl.DeviceIdType.MESH)
+            return 0
+        lax.fori_loop(1, n, one, 0)
+    hello("tp", me, ndev)
+    hello("dp", grp, groups)
+    pl.semaphore_wait(barrier, ndev - 1 + groups - 1)
 
     class Gather:
         def __init__(self, view, ssem, rsem):
             def full(chip):
-                return view(chip, mine)
+                return view(chip, (k, None))
 
             def sibrows(chip):
-                return view(chip, other)
+                return view(chip, (1 - k, None))
 
             def hf(chip, h):
-                return view(chip, my_half(h))
+                return view(chip, (k, h))
 
             def ohf(chip, h):
-                return view(chip, pl.ds(pl.multiple_of((1 - k) * rows + h * half, half), half))
+                return view(chip, (1 - k, h))
 
             self.send = [
                 remote(full(c), full(c), ssem.at[0], rsem.at[0], left),
@@ -189,16 +198,111 @@
     rs_f = Scatter(PF, XF, RF, rs_send.at[0], rs_recv.at[0])
     rs_b = Scatter(PB, XB, RB, rs_send.at[1], rs_recv.at[1])
 
+    def span(r):
+        if r[1] is None:
+            return pl.ds(pl.multiple_of(r[0] * rows, rows), rows)
+        return pl.ds(pl.multiple_of(r[0] * rows + r[1] * half, half), half)
+
     def gather_n(buf, par, i):
-        return Gather(lambda chip, r: buf.at[par, chip, r], ag_send.at[i], ag_recv.at[i])
+        return Gather(lambda chip, r: buf.at[par, chip, span(r)], ag_send.at[i], ag_recv.at[i])
 
     def gather_d(buf, i):
-        return Gather(lambda chip, r: buf.at[chip, r], ag_send.at[i], ag_recv.at[i])
+        return Gather(lambda chip, r: buf.at[chip, span(r)], ag_send.at[i], ag_recv.at[i])
 
     def gather_out(out, i):
         def view(chip, r):
-            return out.at[pl.ds(pl.multiple_of(chip * 2 * rows, rows) + r.start, r.size)]
+            at = span(r)
+            return out.at[pl.ds(pl.multiple_of(chip * 2 * rows, rows) + at.start, at.size)]
         return Gather(view, fg_send.at[i], fg_recv.at[i])
+
+    lanes = 128
+    piece = width * head // (lanes * groups)
+
+    def own_piece_copies(layer):
+        if piece >= head:
+            n = piece // head
+            return [pltpu.make_async_copy(
+                wo_hbm.at[layer, :, pl.ds(pl.multiple_of((grp * n + b) * lanes, lanes), lanes)],
+                VG.at[me, pl.ds(layer * piece + b * head, head)], wl_sem.at[layer * n + b]) for b in range(n)]
+        n = head // piece
+        return [pltpu.make_async_copy(
+            wo_hbm.at[layer, pl.ds(pl.multiple_of(lax.rem(grp, n) * piece, piece), piece),
+                      pl.ds(pl.multiple_of((grp // n) * lanes, lanes), lanes)],
+            VG.at[me, pl.ds(layer * piece, piece)], wl_sem.at[layer])]
+
+    def vg_view(chip, r):
+        dev = 2 * chip + r[0]
+        n = layers * piece
+        if r[1] is None:
+            return VG.at[dev]
+        return VG.at[dev, pl.ds(r[1] * (n // 2), n // 2)]
+
+    def piece_send(layer, d):
+        return pltpu.make_async_remote_copy(
+            src_ref=VG.at[:, pl.ds(layer * piece, piece)], dst_ref=wof_hbm.at[layer, grp],
+            send_sem=wx_send.at[layer, d], recv_sem=wx_recv.at[layer, d],
+            device_id={"dp": lax.rem(grp + d, groups), "tp": me}, device_id_type=pl.DeviceIdType.MESH)
+
+    def piece_keep(layer):
+        return pltpu.make_async_copy(VG.at[:, pl.ds(layer * piece, piece)], wof_hbm.at[layer, grp],
+                                     wx_send.at[layer, 0])
+
+    def pieces_out():
+        for layer in reversed(range(layers)):
+            piece_keep(layer).start()
+
+            def one(d, _):
+                piece_send(layer, d).start()
+                return 0
+            lax.fori_loop(1, groups, one, 0)
+
+    def pieces_sent():
+        for layer in range(layers):
+            def one(d, _):
+                piece_send(layer, d).wait_send()
+                return 0
+            lax.fori_loop(1, groups, one, 0)
+
+    def pieces_in(layer):
+        def one(d, _):
+            pltpu.make_async_remote_copy(
+                src_ref=wof_hbm.at[layer, grp], dst_ref=wof_hbm.at[layer, lax.rem(grp + groups - d, groups)],
+                send_sem=wx_send.at[layer, d], recv_sem=wx_recv.at[layer, d],
+                device_id={"dp": grp, "tp": me}, device_id_type=pl.DeviceIdType.MESH).wait_recv()
+            return 0
+        piece_keep(layer).wait()
+        lax.fori_loop(1, groups, one, 0)
+
+    def wov_copies(layer):
+        if piece >= head:
+            n = piece // head
+            return [pltpu.make_async_copy(wof_hbm.at[layer, g, :, pl.ds(b * head, head)],
+                                          WoV.at[:, :, pl.ds((g * n + b) * lanes, lanes)], wl_sem.at[g * n + b])
+                    for g in range(groups) for b in range(n)]
+        n = head // piece
+        return [pltpu.make_async_copy(wof_hbm.at[layer, g],
+                                      WoV.at[:, pl.ds((g % n) * piece, piece), pl.ds((g // n) * lanes, lanes)],
+                                      wl_sem.at[g]) for g in range(groups)]
+
+    def o_copy(chip, s):
+        return remote(O.at[chip, pl.ds(s * rows, rows)], OF.at[:, pl.ds(pl.multiple_of(me * head, head), head)],
+                      o_send.at[2 * chip + s], o_recv.at[me], 2 * chip + s)
+
+    def o_wait_recv():
+        def one(i, _):
+            src = lax.rem(me + i, ndev)
+            at = OF.at[:, pl.ds(pl.multiple_of(src * head, head), head)]
+            remote(at, at, o_send.at[src], o_recv.at[src], src).wait_recv()
+            return 0
+        lax.fori_loop(1, ndev, one, 0)
+
+    def o_wait_send():
+        def one(i, _):
+            dst = lax.rem(me + i, ndev)
+            at = O.at[dst // 2, pl.ds(pl.multiple_of(lax.rem(dst, 2) * rows, rows), rows)]
+            remote(at, at, o_send.at[dst], o_recv.at[dst], dst).wait_send()
+            return 0
+        lax.fori_loop(1, ndev, one, 0)
 
     def weight_copies(layer, slot):
         pairs = [(src.at[layer], dst.at[slot]) for src, dst in ((wo_hbm, Wo), (wu_hbm, Wu), (wd_hbm, Wd))]
@@ -242,7 +346,14 @@
             prob = e / jnp.sum(e, axis=-1, keepdims=True)
             PROB[chip, at] = prob
             O[chip, at] = mm(prob.astype(BF16), v).astype(BF16)
-        PF[chip] = mm(O[chip], Wo[par])
+
+            @pl.when(2 * chip + s != me)
+            def _():
+                o_copy(chip, s).start()
+
+            @pl.when(2 * chip + s == me)
+            def _():
+                OF[:, pl.ds(pl.multiple_of(me * head, head), head)] = O[chip, at]
 
     def attn_bwd(chip, par):
         grad_o2 = mm_t(D1[chip], Wo[par]).astype(BF16)
@@ -358,58 +469,97 @@
             return 0
         lax.fori_loop(0, NCHIP, body, 0)
 
-    def half_step(ag_n, fin_n, ag_d, fin_d, fwd, bwd, wgrad, has_d):
-        fin_n()
+    def attn_apply(old, new, norm_to):
+        o_wait_recv()
+        tile = width // 4
+
+        def tiles(i, _):
+            at = pl.ds(pl.multiple_of(i * tile, tile), tile)
+            FT[:, at] = mm(OF[...], flat(WoV[:, :, at]))
+            return 0
+        lax.fori_loop(0, 4, tiles, 0)
+
+        def step(r, loc, at):
+            x = old[loc] - FT[loc]
+            new[loc] = x
+            if norm_to is not None:
+                norm_to[c, at] = (x * inv_rms(x)).astype(BF16)
+        own_rows(step)
+        o_wait_send()
+
+    def top_half(layer, par, not_first, last):
+        q = 1 - par
+        ag_n = gather_n(N2, par, 0)
+        ag_d = gather_d(D2, 1)
+        ag_next = gather_n(N1, q, 2)
+        finish_state(rs_f, Y2.at[q], Y2.at[par], N2.at[par])
         ag_n.start()
-        when(has_d, rs_b.send_relay)
+        if not last:
+            for cp in weight_copies(layer - 1, q):
+                cp.start()
+        when(not_first, rs_b.send_relay)
         ag_n.near()
 
         def d_start():
-            fin_d()
+            finish_cot(rs_b, C2, Y2.at[q], D2)
             ag_d.start()
-        when(has_d, d_start)
+        when(not_first, d_start)
+        pieces_in(layer)
+        for cp in wov_copies(layer):
+            cp.start()
         ag_n.far()
         ag_n.finish()
-        partials(rs_f, fwd, True)
-        when(has_d, ag_d.near)
-        rs_f.send_direct()
-        rs_f.send_relay()
+
+        def fwd(j, _):
+            attn_fwd(order(j), par)
+            return 0
+        lax.fori_loop(0, NCHIP, fwd, 0)
+        when(not_first, ag_d.near)
+        for cp in wov_copies(layer):
+            cp.wait()
+        if last:
+            attn_apply(Y1.at[par], Y1.at[q], None)
+        else:
+            attn_apply(Y1.at[par], Y1.at[q], N1.at[q])
+            ag_next.start()
 
         def d_end():
             ag_d.far()
             ag_d.finish()
-        when(has_d, d_end)
-        partials(rs_b, bwd, False)
+        when(not_first, d_end)
+        partials(rs_b, lambda chip: mlp_bwd(chip, par), False)
         rs_b.send_opp()
         rs_b.send_direct()
-        wgrad()
-
-    def stage_attn(layer, par, not_first, last):
+
+    def low_half(layer, par, not_first):
         q = 1 - par
-        if not last:
-            for cp in weight_copies(layer - 1, q):
-                cp.start()
-        half_step(
-            gather_n(N2, par, 0), lambda: finish_state(rs_f, Y2.at[q], Y2.at[par], N2.at[par]),
-            gather_d(D2, 1), lambda: finish_cot(rs_b, C2, Y2.at[q], D2),
-            lambda chip: attn_fwd(chip, par), lambda chip: mlp_bwd(chip, par),
-            lambda: mlp_wgrad(layer, par, not_first), not_first)
-
-    def stage_mlp(layer, par, not_first):
-        q = 1 - par
-
-        def fin():
-            finish_state(rs_f, Y1.at[par], Y1.at[q], N1.at[q])
-            for cp in weight_copies(layer - 1, q):
-                cp.wait()
-        half_step(
-            gather_n(N1, q, 2), fin,
-            gather_d(D1, 3), lambda: finish_cot(rs_b, C1, Y1.at[par], D1),
-            lambda chip: mlp_fwd(chip, q), lambda chip: attn_bwd(chip, par),
-            lambda: attn_wgrad(layer, par, not_first), True)
+        ag_n = gather_n(N1, q, 2)
+        ag_d = gather_d(D1, 3)
+        ag_n.near()
+        mlp_wgrad(layer, par, not_first)
+        rs_b.send_relay()
+        ag_n.far()
+        ag_n.finish()
+        finish_cot(rs_b, C1, Y1.at[par], D1)
+        ag_d.start()
+        for cp in weight_copies(layer - 1, q):
+            cp.wait()
+        partials(rs_f, lambda chip: mlp_fwd(chip, q), True)
+        ag_d.near()
+        rs_f.send_direct()
+        rs_f.send_relay()
+        ag_d.far()
+        ag_d.finish()
+        partials(rs_b, lambda chip: attn_bwd(chip, par), False)
+        rs_b.send_opp()
+        rs_b.send_direct()
+        attn_wgrad(layer, par, not_first)
 
     top = layers - 1
     tp = top % 2
+    for layer in range(layers):
+        for cp in own_piece_copies(layer):
+            cp.start()
     for cp in weight_copies(top, tp):
         cp.start()
     loads = [pltpu.make_async_copy(src.at[me], dst, own_sem.at[i]) for i, (src, dst) in enumerate(
@@ -459,10 +609,19 @@
     lax.fori_loop(0, NCHIP, start_y1, 0)
     for i in range(batch):
         load_c2(0, i).start()
+    ag_w = Gather(vg_view, wg_send, wg_recv)
+    for layer in range(layers):
+        for cp in own_piece_copies(layer):
+            cp.wait()
+    ag_w.start()
     for cp in weight_copies(top, tp):
         cp.wait()
     partials(rs_f, top_fwd, True)
+    ag_w.near()
     rs_f.send_direct()
+    ag_w.far()
+    ag_w.finish()
+    pieces_out()
     cast_c2(0)
     rs_f.send_relay()
     for b in range(1, 2 * NCHIP // batch):
@@ -473,12 +632,12 @@
     def layer_body(i, _):
         layer = top - i
         par = lax.rem(layer, 2)
-        stage_attn(layer, par, layer < top, False)
-        stage_mlp(layer, par, layer < top)
+        top_half(layer, par, layer < top, False)
+        low_half(layer, par, layer < top)
         return 0
     lax.fori_loop(0, top, layer_body, 0)
 
-    stage_attn(0, 0, True, True)
+    top_half(0, 0, True, True)
     outs = [gather_out(o, i) for i, o in enumerate((x1_out, x2_out, g1_out, g2_out))]
 
     def put(i, src):
@@ -494,31 +653,32 @@
         pltpu.make_async_copy(src, out.at[at], own_sem.at[i]).wait()
 
     ag_d1 = gather_d(D1, 3)
-    finish_state(rs_f, Y1.at[0], Y1.at[1], None)
+    put(0, Y1.at[1])
+    mlp_wgrad(0, 0, True)
     rs_b.send_relay()
-    put(1, Y2.at[0])
     finish_cot(rs_b, C1, Y1.at[0], D1)
     ag_d1.start()
-    put(0, Y1.at[1])
+    outs[0].near()
+    put(1, Y2.at[0])
     ag_d1.near()
-    outs[1].near()
     ag_d1.far()
     ag_d1.finish()
     partials(rs_b, lambda chip: attn_bwd(chip, 0), False)
     rs_b.send_opp()
     rs_b.send_direct()
+    outs[1].near()
     put(2, C1)
     attn_wgrad(0, 0, True)
-    outs[0].near()
+    outs[0].far()
     rs_b.send_relay()
     outs[1].far()
     finish_cot(rs_b, C2, Y2.at[0], None)
     put(3, C2)
-    outs[0].far()
     outs[2].near()
     outs[3].near()
     outs[2].far()
     outs[3].far()
+    pieces_sent()
     for i, src in enumerate((Y1.at[1], Y2.at[0], C1, C2)):
         outs[i].finish()
         put_done(i, src)
@@ -530,6 +690,8 @@
     act_spec = P("dp", None, None)
     weight_specs = (P(None, None, "tp", None, None), P(None, "tp", None, None), P(None, None, "tp"), P(None, "tp", None))
     grad_specs = (P("dp", None, "tp", None, None), P("dp", "tp", None, None), P("dp", None, "tp"), P("dp", "tp", None))
+
+    groups = mesh.shape["dp"]
 
     def local_backward(out_y1, out_y2, cot_y1, cot_y2, w_qkv, w_out, w_up, w_down):
         seqs, rows, width = out_y1.shape
@@ -539,17 +701,19 @@
         wo = w_out.reshape(layers, heads * head, width)
         pair = 2 * rows
         qkv_w = three * head
+        piece = width * head // (128 * groups)
         act = jax.ShapeDtypeStruct((seqs * rows, width), F32)
         dma = pltpu.SemaphoreType.DMA
         outs = pl.pallas_call(
-            kernel,
+            functools.partial(kernel, groups),
             out_shape=(act, act, act, act,
                        jax.ShapeDtypeStruct((layers * width * three, head), F32),
                        jax.ShapeDtypeStruct((layers, head, width), F32),
                        jax.ShapeDtypeStruct((layers, width, hidden), F32),
-                       jax.ShapeDtypeStruct((layers, hidden, width), F32)),
+                       jax.ShapeDtypeStruct((layers, hidden, width), F32),
+                       jax.ShapeDtypeStruct((layers, groups, seqs, piece, 128), BF16)),
             in_specs=[pl.BlockSpec(memory_space=pl.ANY)] * 8,
-            out_specs=[pl.BlockSpec(memory_space=pl.ANY)] * 8,
+            out_specs=[pl.BlockSpec(memory_space=pl.ANY)] * 9,
             scratch_shapes=[
                 pltpu.VMEM((2, NCHIP, pair, width), BF16),
                 pltpu.VMEM((2, NCHIP, pair, width), BF16),
@@ -580,8 +744,14 @@
                 pltpu.VMEM((NCHIP, rows, width), BF16),
                 pltpu.VMEM((3, rows, width), F32),
                 pltpu.VMEM((3, rows, width), BF16),
+                pltpu.VMEM((seqs, layers * piece, 128), BF16),
+                pltpu.VMEM((seqs, head, width), BF16),
+                pltpu.VMEM((rows, seqs * head), BF16),
+                pltpu.VMEM((rows, width), F32),
                 dma((4, 9)), dma((4, 9)), dma((2, 10)), dma((2, 10)), dma((4, 9)), dma((4, 9)),
                 dma((2, 6)), dma((4,)), dma((2, NCHIP, 2)), dma((4,)),
+                dma((9,)), dma((9,)), dma((layers, groups)), dma((layers, groups)),
+                dma((max(layers * max(1, piece // head), groups, width // 128),)), dma((seqs,)), dma((seqs,)),
             ],
             compiler_params=pltpu.CompilerParams(collective_id=0, has_side_effects=True,
                                                  vmem_limit_bytes=60 * 1024 * 1024),

time: 461 us -> 450 us (0.976)
  Pallas kernels: 430 us -> 419 us
    pallas_call x1, Pallas kernels: 430 us -> 419 us  [local_backward(): pl.pallas_call(functools.partial(kernel, groups), out_shape=(act, act, ac...]
where the time goes in v3:
time: 450 us
  Pallas kernels  419 us (93%)
  local copies, waits for them, and re-layouts  30.1 us (7%)
    pallas_call x1, Pallas kernels, local_backward(): pl.pallas_call(functools.partial(kernel, groups), out_shape=(act, act, ac...  419 us
    unnamed x28, local copies, waits for them, and re-layouts  30.1 us

profile of v3, /device:TPU:81, one launch (start us, length us, event | category | flops | bytes accessed | tf_op | source)
XLA Modules:
  0.0 449.6 jit_solution(17663230988289431590)
XLA Ops:
  0.6 418.8 %shard_map.143 = (f32[1024,1024]{1,0:T(8,128)}, f32[1024,1024]{1,0:T(8,128)}, f32[1024,1024]{1,0:T(8,128)}, f32[1024,1024]{1,0:T(8,128)}, f32[12288,128]{1,0:T(8...) custom-call(f32[8,128,1024]{2,1,0:T(8,128)} %y1_hbm.1, ...), custom_call_target="tpu_custom_call" | custom-call | tf_op jit(solution)/shard_map/pallas_call | solution.py:707
  419.4 0.0 copy-start.2
  419.4 4.9 %copy.28 = f32[8,128,1024]{2,1,0:T(8,128)} copy(f32[8,128,1024]{2,1,0:T(8,128)} %bitcast.22) | data formatting | bytes 8388608
  424.4 0.0 copy-done.2
  424.4 0.0 copy-start.1
  424.4 0.0 slice-start.4
  424.4 2.1 copy.29
  426.5 1.6 copy-done.1
  428.1 0.0 copy-start
  428.1 0.0 slice-start.5
  428.1 2.1 copy.30
  430.2 1.8 copy-done
  432.1 0.0 slice-start.2
  432.1 2.1 copy.31
  434.2 0.0 slice-done.4
  434.2 0.0 slice-done.5
  434.2 0.0 copy-start.3
  434.2 0.0 slice-start.3
  434.2 3.2 copy.32
  437.4 1.2 copy-done.3
  438.6 0.0 slice-start
  438.6 1.3 copy.33
  440.0 0.0 slice-done.2
  440.0 0.5 slice-done.3
  440.5 0.0 slice-start.1
  440.5 4.3 copy.34
  444.8 0.0 slice-done
  444.8 1.4 slice-done.1
  446.2 3.4 copy.35
  (3 shorter events, 0.0 us)
Async XLA Ops:
  419.4 5.0 %copy-start.2 = (f32[1024,1024]{1,0:T(8,128)S(1)}, f32[1024,1024]{1,0:T(8,128)}, u32[]{:S(2)}) copy-start(f32[1024,1024]{1,0:T(8,128)} %get-tuple-element.17) | copy-start | bytes 12582916
  424.4 3.7 copy-start.1
  424.4 9.8 %slice-start.4 = ((s8[6291456]{0:T(1024)(128)(4,1)}), s8[4194304]{0:T(1024)(128)(4,1)S(1)}, s32[]{:S(2)}) async-start(s8[6291456]{0:T(1024)(128)(4,1)} %bitcast.16), calls=%async_computation.4 | async-start | bytes 8388608
  428.1 4.0 copy-start
  428.1 6.1 %slice-start.5 = ((s8[6291456]{0:T(1024)(128)(4,1)}), s8[2097152]{0:T(1024)(128)(4,1)S(1)}, s32[]{:S(2)}) async-start(s8[6291456]{0:T(1024)(128)(4,1)} %bitcast.16), calls=%async_computation.5 | async-start | bytes 4194304
  432.1 7.9 %slice-start.2 = ((s8[8388608]{0:T(1024)(128)(4,1)}), s8[4194304]{0:T(1024)(128)(4,1)S(1)}, s32[]{:S(2)}) async-start(s8[8388608]{0:T(1024)(128)(4,1)} %bitcast.14), calls=%async_computation.2 | async-start | bytes 8388608
  434.2 4.4 copy-start.3
  434.2 6.3 %slice-start.3 = ((s8[8388608]{0:T(1024)(128)(4,1)}), s8[4194304]{0:T(1024)(128)(4,1)S(1)}, s32[]{:S(2)}) async-start(s8[8388608]{0:T(1024)(128)(4,1)} %bitcast.14), calls=%async_computation.3 | async-start | bytes 8388608
  438.6 6.1 %slice-start = ((s8[8388608]{0:T(1024)(128)(4,1)}), s8[4194304]{0:T(1024)(128)(4,1)S(1)}, s32[]{:S(2)}) async-start(s8[8388608]{0:T(1024)(128)(4,1)} %bitcast.12), calls=%async_computation | async-start | bytes 8388608
  440.5 5.7 %slice-start.1 = ((s8[8388608]{0:T(1024)(128)(4,1)}), s8[4194304]{0:T(1024)(128)(4,1)S(1)}, s32[]{:S(2)}) async-start(s8[8388608]{0:T(1024)(128)(4,1)} %bitcast.12), calls=%async_computation.1 | async-start | bytes 8388608

commit v4 on v3

v4 whole, which is shorter than its diff:
```python
import functools
import math
import jax
import jax.numpy as jnp
from jax import lax
from jax.experimental import pallas as pl
from jax.experimental.pallas import tpu as pltpu
from jax.sharding import PartitionSpec as P

NORM_EPS = 1e-6
F32, BF16 = jnp.float32, jnp.bfloat16
GELU_C = math.sqrt(2.0 / math.pi)
GELU_A = 0.044715
NCHIP = 4


def mm(a, b):
    return lax.dot_general(a, b, (((1,), (0,)), ((), ())), preferred_element_type=F32)


def mm_t(a, b):
    return lax.dot_general(a, b, (((1,), (1,)), ((), ())), preferred_element_type=F32)


def tmm(a, b):
    return lax.dot_general(a, b, (((0,), (0,)), ((), ())), preferred_element_type=F32)


def kernel(groups, y1_hbm, y2_hbm, c1_hbm, c2_hbm, wqkv_hbm, wo_hbm, wu_hbm, wd_hbm,
           x1_out, x2_out, g1_out, g2_out, gqkv_out, gout_out, gup_out, gdown_out, wof_hbm,
           N1, N2, D1, D2, Wqkv, Wo, Wu, Wd, SQ, SO, SU, SD, H, ACT, GH, QKV, PROB, OG, GQ,
           Y1, Y2, C1, C2, PF, PB, XF, XB, RF, RB, VG, WoV,
           ag_send, ag_recv, rs_send, rs_recv, fg_send, fg_recv, w_sem, g_sem, io_sem, own_sem,
           wg_send, wg_recv, wx_send, wx_recv, wl_sem):
    layers = wqkv_hbm.shape[0]
    rows = y1_hbm.shape[1]
    half = rows // 2
    width = y1_hbm.shape[2]
    head = wo_hbm.shape[1]
    scale = 1.0 / math.sqrt(head)
    ndev = 2 * NCHIP
    me = lax.axis_index("tp")
    c = me // 2
    k = lax.rem(me, 2)
    sib = me + 1 - 2 * k
    left = lax.rem(me + ndev - 2, ndev)
    right = lax.rem(me + 2, ndev)
    cl = lax.rem(c + NCHIP - 1, NCHIP)
    cr = lax.rem(c + 1, NCHIP)
    co = lax.rem(c + 2, NCHIP)
    mine = pl.ds(pl.multiple_of(k * rows, rows), rows)
    other = pl.ds(pl.multiple_of((1 - k) * rows, rows), rows)

    def my_half(h):
        return pl.ds(pl.multiple_of(k * rows + h * half, half), half)

    def order(j):
        off = (2 + j) * (1 - j // 2) + (3 - j) * (j // 2)
        return lax.rem(c + off, NCHIP)

    def remote(src, dst, ssem, rsem, dev):
        return pltpu.make_async_remote_copy(src_ref=src, dst_ref=dst, send_sem=ssem, recv_sem=rsem,
                                            device_id={"tp": dev}, device_id_type=pl.DeviceIdType.MESH)

    grp = lax.axis_index("dp")
    barrier = pltpu.get_barrier_semaphore()

    def hello(axis, at, n):
        def one(i, _):
            pl.semaphore_signal(barrier, inc=1, device_id={axis: lax.rem(at + i, n)},
                                device_id_type=pl.DeviceIdType.MESH)
            return 0
        lax.fori_loop(1, n, one, 0)
    hello("tp", me, ndev)
    hello("dp", grp, groups)
    pl.semaphore_wait(barrier, ndev - 1 + groups - 1)

    class Gather:
        def __init__(self, view, ssem, rsem, own=None):
            src = (lambda h: view(c, k, h)) if own is None else own
            moves = [(src(h), view(c, k, h), dev) for h in (0, 1) for dev in (left, right, sib)]
            moves += [(view(chip, k, h), view(chip, k, h), dev) for chip, h, dev in (
                (cr, 0, left), (cl, 1, right), (cr, 0, sib), (cl, 0, sib), (cr, 1, sib), (cl, 1, sib),
                (co, 0, sib), (co, 1, sib))]
            self.send = [remote(a, b, ssem.at[i], rsem.at[i], dev) for i, (a, b, dev) in enumerate(moves)]
            o = 1 - k
            land = [(cr, k, 0), (cl, k, 0), (c, o, 0), (cr, k, 1), (cl, k, 1), (c, o, 1), (co, k, 0), (co, k, 1),
                    (cr, o, 0), (cl, o, 0), (cr, o, 1), (cl, o, 1), (co, o, 0), (co, o, 1)]
            self.recv = [remote(view(*at), view(*at), ssem.at[i], rsem.at[i], sib) for i, at in enumerate(land)]

        def pass_on(self, got, *sends):
            self.recv[got].wait_recv()
            for i in sends:
                self.send[i].start()

        def start_half(self, h):
            for i in range(3 * h, 3 * h + 3):
                self.send[i].start()

        def start(self):
            self.start_half(0)
            self.start_half(1)

        def near0(self):
            self.pass_on(0, 6, 8)
            self.pass_on(1, 9)

        def near1(self):
            self.pass_on(4, 7, 11)
            self.pass_on(3, 10)

        def near(self):
            self.near0()
            self.near1()

        def far(self):
            self.pass_on(6, 12)
            self.pass_on(7, 13)

        def finish(self):
            for i in (2, 5, 8, 9, 10, 11, 12, 13):
                self.recv[i].wait_recv()
            for cp in self.send:
                cp.wait_send()

    class Scatter:
        def __init__(self, part, from_sib, rec, ssem, rsem):
            self.part, self.from_sib = part, from_sib
            self.rel, self.dir, self.fin = rec.at[0], rec.at[1], rec.at[2]
            self.ssem, self.rsem = ssem, rsem

            def hp(chip, h):
                return part.at[chip, my_half(h)]

            def hr(buf, h):
                return buf.at[pl.ds(h * half, half)]

            def mk(i, src, dst, dev):
                return remote(src, dst, ssem.at[i], rsem.at[i], dev)

            self.opp = [mk(4, hp(co, 0), hr(self.rel, 0), left), mk(5, hp(co, 1), hr(self.rel, 1), right)]
            self.direct = [mk(6, hp(cl, 1), hr(self.dir, 1), left), mk(7, hp(cr, 0), hr(self.dir, 0), right)]
            self.relay = [mk(8, hp(cl, 0), hr(self.fin, 0), left), mk(9, hp(cr, 1), hr(self.fin, 1), right)]

        def pair(self, chip):
            return remote(self.part.at[chip, other], self.from_sib.at[chip], self.ssem.at[chip],
                          self.rsem.at[chip], sib)

        def add(self, chip):
            self.pair_recv(chip)
            got = self.part[chip, mine].astype(F32) + self.from_sib[chip].astype(F32)
            self.part[chip, mine] = got.astype(self.part.dtype)

        def pair_recv(self, chip):
            remote(self.from_sib.at[chip], self.from_sib.at[chip], self.ssem.at[chip], self.rsem.at[chip],
                   sib).wait_recv()

        def send_opp(self):
            self.add(co)
            for cp in self.opp:
                cp.start()

        def send_direct(self):
            self.add(cl)
            self.direct[0].start()
            self.add(cr)
            self.direct[1].start()

        def send_relay(self):
            for h, (chip, cp) in enumerate(((cl, self.relay[0]), (cr, self.relay[1]))):
                self.opp[h].wait_recv()
                got = self.part[chip, my_half(h)].astype(F32) + self.rel[h * half:(h + 1) * half].astype(F32)
                self.part[chip, my_half(h)] = got.astype(self.part.dtype)
                cp.start()

        def land(self):
            self.pair_recv(c)
            for cp in self.direct + self.relay:
                cp.wait_recv()

        def total(self, r):
            at = pl.ds(pl.multiple_of(k * rows + r * 16, 16), 16)
            loc = pl.ds(pl.multiple_of(r * 16, 16), 16)
            return (self.part[c, at].astype(F32) + self.from_sib[c, loc].astype(F32)
                    + self.fin[loc].astype(F32) + self.dir[loc].astype(F32))

        def drain(self):
            for chip in range(NCHIP):
                self.pair(chip).wait_send()
            for cp in self.opp + self.direct + self.relay:
                cp.wait_send()

    rs_f = Scatter(PF, XF, RF, rs_send.at[0], rs_recv.at[0])
    rs_b = Scatter(PB, XB, RB, rs_send.at[1], rs_recv.at[1])

    def span(core, h):
        return pl.ds(pl.multiple_of(core * rows + h * half, half), half)

    def gather_rows(buf, i):
        return Gather(lambda chip, core, h: buf.at[chip, span(core, h)], ag_send.at[i], ag_recv.at[i])

    def heads_of(chip, core):
        return pl.ds(pl.multiple_of((2 * chip + core) * head, head), head)

    def gather_o():
        n = NCHIP // 2
        return Gather(lambda chip, core, h: OG.at[pl.ds(h * n, n), :, heads_of(chip, core)],
                      ag_send.at[3], ag_recv.at[3])

    def gather_out(out, i, src):
        def view(chip, core, h):
            return out.at[pl.ds(pl.multiple_of((2 * chip + core) * rows + h * half, half), half)]
        return Gather(view, fg_send.at[i], fg_recv.at[i], lambda h: src.at[pl.ds(h * half, half)])

    def keep_out(out, i, src):
        return pltpu.make_async_copy(src, out.at[pl.ds(pl.multiple_of(me * rows, rows), rows)], own_sem.at[i])

    lanes = 128
    piece = width * head // (lanes * groups)

    def own_piece_copies(layer):
        if piece >= head:
            n = piece // head
            return [pltpu.make_async_copy(
                wo_hbm.at[layer, :, pl.ds(pl.multiple_of((grp * n + b) * lanes, lanes), lanes)],
                VG.at[me, pl.ds(layer * piece + b * head, head)], wl_sem.at[layer * n + b]) for b in range(n)]
        n = head // piece
        return [pltpu.make_async_copy(
            wo_hbm.at[layer, pl.ds(pl.multiple_of(lax.rem(grp, n) * piece, piece), piece),
                      pl.ds(pl.multiple_of((grp // n) * lanes, lanes), lanes)],
            VG.at[me, pl.ds(layer * piece, piece)], wl_sem.at[layer])]

    def vg_view(chip, core, h):
        n = layers * piece // 2
        return VG.at[2 * chip + core, pl.ds(h * n, n)]

    def piece_send(layer, d):
        return pltpu.make_async_remote_copy(
            src_ref=VG.at[:, pl.ds(layer * piece, piece)], dst_ref=wof_hbm.at[layer, grp],
            send_sem=wx_send.at[layer, d], recv_sem=wx_recv.at[layer, d],
            device_id={"dp": lax.rem(grp + d, groups), "tp": me}, device_id_type=pl.DeviceIdType.MESH)

    def piece_keep(layer):
        return pltpu.make_async_copy(VG.at[:, pl.ds(layer * piece, piece)], wof_hbm.at[layer, grp],
                                     wx_send.at[layer, 0])

    def pieces_out():
        for layer in reversed(range(layers)):
            piece_keep(layer).start()

            def one(d, _):
                piece_send(layer, d).start()
                return 0
            lax.fori_loop(1, groups, one, 0)

    def pieces_sent():
        for layer in range(layers):
            def one(d, _):
                piece_send(layer, d).wait_send()
                return 0
            lax.fori_loop(1, groups, one, 0)

    def pieces_in(layer):
        def one(d, _):
            pltpu.make_async_remote_copy(
                src_ref=wof_hbm.at[layer, grp], dst_ref=wof_hbm.at[layer, lax.rem(grp + groups - d, groups)],
                send_sem=wx_send.at[layer, d], recv_sem=wx_recv.at[layer, d],
                device_id={"dp": grp, "tp": me}, device_id_type=pl.DeviceIdType.MESH).wait_recv()
            return 0
        piece_keep(layer).wait()
        lax.fori_loop(1, groups, one, 0)

    def wov_copies(layer):
        if piece >= head:
            n = piece // head
            return [pltpu.make_async_copy(wof_hbm.at[layer, g, :, pl.ds(b * head, head)],
                                          WoV.at[:, :, pl.ds((g * n + b) * lanes, lanes)], wl_sem.at[g * n + b])
                    for g in range(groups) for b in range(n)]
        n = head // piece
        return [pltpu.make_async_copy(wof_hbm.at[layer, g],
                                      WoV.at[:, pl.ds((g % n) * piece, piece), pl.ds((g // n) * lanes, lanes)],
                                      wl_sem.at[g]) for g in range(groups)]

    def weight_copies(layer, slot):
        pairs = [(src.at[layer], dst.at[slot]) for src, dst in ((wo_hbm, Wo), (wu_hbm, Wu), (wd_hbm, Wd))]
        pairs += [(wqkv_hbm.at[layer, j], Wqkv.at[slot, :, pl.ds(j * head, head)]) for j in range(3)]
        return [pltpu.make_async_copy(src, dst, w_sem.at[slot, i]) for i, (src, dst) in enumerate(pairs)]

    tile = width // 4

    def grad_copy(layer, i, t):
        at = pl.ds(pl.multiple_of(t * tile, tile), tile)
        if i == 0:
            size = 3 * width
            dst = gqkv_out.at[pl.ds(pl.multiple_of(layer * size + t * 3 * tile, 3 * tile), 3 * tile)]
        else:
            dst = (gout_out.at[layer, :, at], gup_out.at[layer, at], gdown_out.at[layer, :, at])[i - 1]
        return pltpu.make_async_copy((SQ, SO, SU, SD)[i].at[lax.rem(t, 2)], dst, g_sem.at[i, lax.rem(t, 2)])

    def wgrad_tiles(layer, i, fill):
        def body(t, _):
            pl.when(t >= 2)(lambda: grad_copy(layer, i, t - 2).wait())
            fill(t, lax.rem(t, 2), pl.ds(pl.multiple_of(t * tile, tile), tile))
            grad_copy(layer, i, t).start()
            return 0
        lax.fori_loop(0, 4, body, 0)

    def wgrad_wait(layer, i):
        for t in (2, 3):
            grad_copy(layer, i, t).wait()

    def mlp_fwd(chip, par):
        hid = mm(N1[par, chip], Wu[par])
        H[chip] = hid
        act = hid * (0.5 * (1.0 + jnp.tanh(GELU_C * (hid + GELU_A * (hid * hid * hid)))))
        act = act.astype(BF16)
        ACT[par, chip] = act
        PF[chip] = mm(act, Wd[par])

    def mlp_bwd(chip, par):
        grad_act = mm_t(D2[chip], Wd[par])
        hid = H[chip]
        sq = hid * hid
        t = jnp.tanh(GELU_C * (hid + GELU_A * (sq * hid)))
        slope = 0.5 * (1.0 + t) + (0.5 * hid) * ((1.0 - t * t) * (GELU_C * (1.0 + (3.0 * GELU_A) * sq)))
        grad_hid = (grad_act * slope).astype(BF16)
        GH[chip] = grad_hid
        PB[chip] = mm_t(grad_hid, Wu[par]).astype(BF16)

    def attn_fwd(chip, par):
        QKV[chip] = mm(N2[par, chip], Wqkv[par]).astype(BF16)
        for s in range(2):
            at = slice(s * rows, (s + 1) * rows)
            q = QKV[chip, at, 0:head]
            kk = QKV[chip, at, head:2 * head]
            v = QKV[chip, at, 2 * head:3 * head]
            sc = mm_t(q, kk) * scale
            e = jnp.exp(sc - jnp.max(sc, axis=-1, keepdims=True))
            prob = e / jnp.sum(e, axis=-1, keepdims=True)
            PROB[chip, at] = prob
            OG[chip, at, heads_of(c, k)] = mm(prob.astype(BF16), v).astype(BF16)

    def attn_bwd(chip, par):
        grad_o2 = mm_t(D1[chip], Wo[par]).astype(BF16)
        for s in range(2):
            at = slice(s * rows, (s + 1) * rows)
            grad_o = grad_o2[at]
            q = QKV[chip, at, 0:head]
            kk = QKV[chip, at, head:2 * head]
            v = QKV[chip, at, 2 * head:3 * head]
            prob = PROB[chip, at]
            grad_p = mm_t(grad_o, v)
            grad_s = (prob * (grad_p - jnp.sum(grad_p * prob, axis=-1, keepdims=True)) * scale).astype(BF16)
            GQ[chip, at, 0:head] = mm(grad_s, kk).astype(BF16)
            GQ[chip, at, head:2 * head] = tmm(grad_s, q).astype(BF16)
            GQ[chip, at, 2 * head:3 * head] = tmm(prob.astype(BF16), grad_o).astype(BF16)
        PB[chip] = mm_t(GQ[chip], Wqkv[par]).astype(BF16)

    def flat(x):
        return x.reshape((x.shape[0] * x.shape[1],) + x.shape[2:])

    def mlp_wgrad(layer, par):
        def up(t, slot, at):
            SU[slot] = tmm(flat(N1[par, :, :, at]), flat(GH[...]))

        def down(t, slot, at):
            SD[slot] = tmm(flat(ACT[par]), flat(D2[:, :, at]))
        wgrad_tiles(layer, 2, up)
        wgrad_tiles(layer, 3, down)
        wgrad_wait(layer, 2)
        wgrad_wait(layer, 3)

    def attn_wgrad(layer, par):
        def qkv(t, slot, at):
            res = tmm(flat(N2[par, :, :, at]), flat(GQ[...]))
            for j in range(3):
                SQ[slot, pl.ds(j, tile, stride=3), :] = res[:, j * head:(j + 1) * head]

        def out(t, slot, at):
            SO[slot] = tmm(flat(OG[:, :, heads_of(c, k)]), flat(D1[:, :, at]))
        wgrad_tiles(layer, 0, qkv)
        wgrad_tiles(layer, 1, out)
        wgrad_wait(layer, 0)
        wgrad_wait(layer, 1)

    def own_rows(step):
        def body(r, _):
            step(r, pl.ds(pl.multiple_of(r * 16, 16), 16), pl.ds(pl.multiple_of(k * rows + r * 16, 16), 16))
            return 0
        lax.fori_loop(0, rows // 16, body, 0)

    def inv_rms(x):
        return lax.rsqrt(jnp.mean(x * x, axis=-1, keepdims=True) + NORM_EPS)

    def finish_state(rs, old, new, norm_to):
        rs.land()

        def step(r, loc, at):
            x = old[loc] - rs.total(r)
            new[loc] = x
            if norm_to is not None:
                norm_to[c, at] = (x * inv_rms(x)).astype(BF16)
        own_rows(step)
        rs.drain()

    def finish_cot(rs, cot, x_ref, cast_to):
        rs.land()

        def step(r, loc, at):
            x = x_ref[loc]
            inv = inv_rms(x)
            normed = x * inv
            grad_n = rs.total(r)
            new = cot[loc] + inv * (grad_n - normed * jnp.mean(normed * grad_n, axis=-1, keepdims=True))
            cot[loc] = new
            if cast_to is not None:
                cast_to[c, at] = new.astype(BF16)
        own_rows(step)
        rs.drain()

    def finish_sum(rs, to):
        rs.land()

        def step(r, loc, at):
            to[c, at] = rs.total(r).astype(BF16)
        own_rows(step)
        rs.drain()

    def chip_rows(step):
        def body(i, _):
            step(pl.ds(pl.multiple_of(i * 16, 16), 16))
            return 0
        lax.fori_loop(0, 2 * rows // 16, body, 0)

    def attn_apply(chip, par):
        q = 1 - par
        PF[chip] = mm(OG[chip], flat(WoV[...]))

        def step(at):
            x = Y1[par, chip, at] - PF[chip, at]
            Y1[q, chip, at] = x
            N1[q, chip, at] = (x * inv_rms(x)).astype(BF16)
        chip_rows(step)

    def cot_apply(chip, par):
        def step(at):
            x = Y1[par, chip, at]
            inv = inv_rms(x)
            normed = x * inv
            grad_n = D1[chip, at].astype(F32)
            new = C1[chip, at] + inv * (grad_n - normed * jnp.mean(normed * grad_n, axis=-1, keepdims=True))
            C1[chip, at] = new
            D1[chip, at] = new.astype(BF16)
        chip_rows(step)

    def when(cond, fn):
        if cond is True:
            fn()
        elif cond is not False:
            pl.when(cond)(fn)

    def partials(rs, compute, extra=()):
        def body(j, _):
            chip = order(j)
            compute(chip)
            rs.pair(chip).start()
            for at, fn in extra:
                pl.when(j == at)(fn)
            return 0
        lax.fori_loop(0, NCHIP, body, 0)

    def top_half(layer, par, not_first, last):
        q = 1 - par
        ag_d = gather_rows(D2, 1)
        ag_o = gather_o()
        if last:
            ag_n = gather_out(x2_out, 0, Y2.at[par])
            finish_state(rs_f, Y2.at[q], Y2.at[par], None)
            ag_n.start()
            keep_out(x2_out, 0, Y2.at[par]).start()
        else:
            ag_n = gather_rows(N2.at[par], 0)
            finish_state(rs_f, Y2.at[q], Y2.at[par], N2.at[par])
            ag_n.start()
            for cp in weight_copies(layer - 1, q):
                cp.start()
        when(not_first, rs_b.send_relay)
        ag_n.near()

        def d_start():
            attn_wgrad(layer + 1, q)
            finish_cot(rs_b, C2, Y2.at[q], D2)
            ag_d.start()
        when(not_first, d_start)
        ag_n.far()
        ag_n.finish()
        if last:
            keep_out(x2_out, 0, Y2.at[par]).wait()
            loads = [pltpu.make_async_copy(x2_out.at[pl.ds(chip * 2 * rows, 2 * rows)], PF.at[chip],
                                           io_sem.at[0, chip, 0]) for chip in range(NCHIP)]
            for cp in loads:
                cp.start()
            for chip in range(NCHIP):
                loads[chip].wait()

                def step(at):
                    x = PF[chip, at]
                    N2[par, chip, at] = (x * inv_rms(x)).astype(BF16)
                chip_rows(step)
        pieces_in(layer)
        for cp in wov_copies(layer):
            cp.start()

        def fwd(chip, _):
            attn_fwd(chip, par)

            @pl.when(chip == NCHIP // 2 - 1)
            def _():
                ag_o.start_half(0)
                when(not_first, ag_d.near)
            return 0
        lax.fori_loop(0, NCHIP, fwd, 0)
        ag_o.start_half(1)
        ag_o.near0()

        def d_end():
            ag_d.far()
            ag_d.finish()
        when(not_first, d_end)
        partials(rs_b, lambda chip: mlp_bwd(chip, par), ((0, ag_o.near1), (1, rs_b.send_opp)))
        rs_b.send_direct()
        for cp in wov_copies(layer):
            cp.wait()
        ag_o.far()
        ag_o.finish()

    def low_half(layer, par):
        q = 1 - par
        ag_d = gather_rows(D1, 2)
        for cp in weight_copies(layer - 1, q):
            cp.wait()

        def fwd(chip):
            attn_apply(chip, par)
            mlp_fwd(chip, q)
        partials(rs_f, fwd, ((0, rs_b.send_relay), (1, rs_f.send_opp)))
        finish_sum(rs_b, D1)
        ag_d.start()
        rs_f.send_direct()
        mlp_wgrad(layer, par)
        ag_d.near()
        rs_f.send_relay()
        ag_d.far()
        ag_d.finish()
        attn_back(par)

    def attn_back(par):
        def bwd(chip):
            cot_apply(chip, par)
            attn_bwd(chip, par)
        partials(rs_b, bwd, ((1, rs_b.send_opp),))
        rs_b.send_direct()

    top = layers - 1
    tp = top % 2
    for layer in range(layers):
        for cp in own_piece_copies(layer):
            cp.start()
    for cp in weight_copies(top, tp):
        cp.start()
    loads = [pltpu.make_async_copy(src.at[me], dst, own_sem.at[i]) for i, (src, dst) in enumerate(
        ((y2_hbm, Y2.at[1 - tp]), (c2_hbm, C2)))]
    for cp in loads:
        cp.start()

    def load_rows(src, dst, i, chip, s):
        return pltpu.make_async_copy(src.at[2 * chip + s], dst.at[chip, pl.ds(s * rows, rows)], io_sem.at[i, chip, s])

    def each_pair(fn):
        def body(j, _):
            for s in range(2):
                fn(order(j), s)
            return 0
        lax.fori_loop(0, NCHIP, body, 0)

    def top_fwd(chip):
        for s in range(2):
            load_rows(y1_hbm, Y1.at[tp], 0, chip, s).wait()

        def step(at):
            x = Y1[tp, chip, at]
            N1[tp, chip, at] = (x * inv_rms(x)).astype(BF16)
        chip_rows(step)
        mlp_fwd(chip, tp)

    def cast_c2():
        each_pair(lambda chip, s: load_rows(c2_hbm, C1, 1, chip, s).wait())

        def body(chip, _):
            def step(at):
                D2[chip, at] = C1[chip, at].astype(BF16)
            chip_rows(step)
            return 0
        lax.fori_loop(0, NCHIP, body, 0)
        each_pair(lambda chip, s: load_rows(c1_hbm, C1, 1, chip, s).start())

    each_pair(lambda chip, s: load_rows(y1_hbm, Y1.at[tp], 0, chip, s).start())
    each_pair(lambda chip, s: load_rows(c2_hbm, C1, 1, chip, s).start())
    ag_w = Gather(vg_view, wg_send, wg_recv)
    for layer in range(layers):
        for cp in own_piece_copies(layer):
            cp.wait()
    ag_w.start()
    for cp in weight_copies(top, tp):
        cp.wait()
    partials(rs_f, top_fwd, ((1, rs_f.send_opp),))
    ag_w.near()
    rs_f.send_direct()
    ag_w.far()
    ag_w.finish()
    pieces_out()
    rs_f.send_relay()
    cast_c2()
    for cp in loads:
        cp.wait()
    each_pair(lambda chip, s: load_rows(c1_hbm, C1, 1, chip, s).wait())

    def layer_body(i, _):
        layer = top - i
        par = lax.rem(layer, 2)
        top_half(layer, par, layer < top, False)
        low_half(layer, par)
        return 0
    lax.fori_loop(0, top, layer_body, 0)

    top_half(0, 0, True, True)
    def put_x1(chip):
        return pltpu.make_async_copy(Y1.at[1, chip], x1_out.at[pl.ds(pl.multiple_of(chip * 2 * rows, rows), 2 * rows)],
                                     io_sem.at[0, chip, 0])

    def put_g1(chip):
        return pltpu.make_async_copy(C1.at[chip], g1_out.at[pl.ds(pl.multiple_of(chip * 2 * rows, rows), 2 * rows)],
                                     io_sem.at[0, chip, 1])

    def x1_rows(chip, _):
        attn_apply(chip, 0)
        put_x1(chip).start()
        return 0

    def each_chip(fn):
        def body(chip, _):
            fn(chip)
            return 0
        lax.fori_loop(0, NCHIP, body, 0)

    ag_d1 = gather_rows(D1, 2)
    rs_b.send_relay()
    finish_sum(rs_b, D1)
    ag_d1.start()
    lax.fori_loop(0, NCHIP, x1_rows, 0)
    ag_d1.near()
    mlp_wgrad(0, 0)
    ag_d1.far()
    ag_d1.finish()
    attn_back(0)
    each_chip(lambda chip: put_g1(chip).start())
    rs_b.send_relay()
    attn_wgrad(0, 0)
    finish_cot(rs_b, C2, Y2.at[0], None)
    last = gather_out(g2_out, 1, C2)
    last.start()
    keep_out(g2_out, 1, C2).start()
    last.near()
    last.far()
    each_chip(lambda chip: put_x1(chip).wait())
    each_chip(lambda chip: put_g1(chip).wait())
    pieces_sent()
    keep_out(g2_out, 1, C2).wait()
    last.finish()


def solution(mesh):
    act_spec = P("dp", None, None)
    weight_specs = (P(None, None, "tp", None, None), P(None, "tp", None, None), P(None, None, "tp"), P(None, "tp", None))
    grad_specs = (P("dp", None, "tp", None, None), P("dp", "tp", None, None), P("dp", None, "tp"), P("dp", "tp", None))

    groups = mesh.shape["dp"]

    def local_backward(out_y1, out_y2, cot_y1, cot_y2, w_qkv, w_out, w_up, w_down):
        seqs, rows, width = out_y1.shape
        layers, _, heads, three, head = w_qkv.shape
        hidden = w_up.shape[2]
        wq = jnp.transpose(w_qkv.reshape(layers, width, three, head), (0, 2, 1, 3))
        wo = w_out.reshape(layers, heads * head, width)
        pair = 2 * rows
        qkv_w = three * head
        piece = width * head // (128 * groups)
        act = jax.ShapeDtypeStruct((seqs * rows, width), F32)
        dma = pltpu.SemaphoreType.DMA
        outs = pl.pallas_call(
            functools.partial(kernel, groups),
            out_shape=(act, act, act, act,
                       jax.ShapeDtypeStruct((layers * width * three, head), F32),
                       jax.ShapeDtypeStruct((layers, head, width), F32),
                       jax.ShapeDtypeStruct((layers, width, hidden), F32),
                       jax.ShapeDtypeStruct((layers, hidden, width), F32),
                       jax.ShapeDtypeStruct((layers, groups, seqs, piece, 128), BF16)),
            in_specs=[pl.BlockSpec(memory_space=pl.ANY)] * 8,
            out_specs=[pl.BlockSpec(memory_space=pl.ANY)] * 9,
            scratch_shapes=[
                pltpu.VMEM((2, NCHIP, pair, width), BF16),
                pltpu.VMEM((2, NCHIP, pair, width), BF16),
                pltpu.VMEM((NCHIP, pair, width), BF16),
                pltpu.VMEM((NCHIP, pair, width), BF16),
                pltpu.VMEM((2, width, qkv_w), BF16),
                pltpu.VMEM((2, head, width), BF16),
                pltpu.VMEM((2, width, hidden), BF16),
                pltpu.VMEM((2, hidden, width), BF16),
                pltpu.VMEM((2, width // 4 * three, head), F32),
                pltpu.VMEM((2, head, width // 4), F32),
                pltpu.VMEM((2, width // 4, hidden), F32),
                pltpu.VMEM((2, hidden, width // 4), F32),
                pltpu.VMEM((NCHIP, pair, hidden), F32),
                pltpu.VMEM((2, NCHIP, pair, hidden), BF16),
                pltpu.VMEM((NCHIP, pair, hidden), BF16),
                pltpu.VMEM((NCHIP, pair, qkv_w), BF16),
                pltpu.VMEM((NCHIP, pair, rows), F32),
                pltpu.VMEM((NCHIP, pair, seqs * head), BF16),
                pltpu.VMEM((NCHIP, pair, qkv_w), BF16),
                pltpu.VMEM((2, NCHIP, pair, width), F32),
                pltpu.VMEM((2, rows, width), F32),
                pltpu.VMEM((NCHIP, pair, width), F32),
                pltpu.VMEM((rows, width), F32),
                pltpu.VMEM((NCHIP, pair, width), F32),
                pltpu.VMEM((NCHIP, pair, width), BF16),
                pltpu.VMEM((NCHIP, rows, width), F32),
                pltpu.VMEM((NCHIP, rows, width), BF16),
                pltpu.VMEM((3, rows, width), F32),
                pltpu.VMEM((3, rows, width), BF16),
                pltpu.VMEM((seqs, layers * piece, 128), BF16),
                pltpu.VMEM((seqs, head, width), BF16),
                dma((4, 14)), dma((4, 14)), dma((2, 10)), dma((2, 10)), dma((2, 14)), dma((2, 14)),
                dma((2, 6)), dma((4, 2)), dma((2, NCHIP, 2)), dma((2,)),
                dma((14,)), dma((14,)), dma((layers, groups)), dma((layers, groups)),
                dma((max(layers * max(1, piece // head), groups, width // 128),)),
            ],
            compiler_params=pltpu.CompilerParams(collective_id=0, has_side_effects=True,
                                                 vmem_limit_bytes=67043328),
        )(out_y1, out_y2, cot_y1, cot_y2, wq, wo, w_up, w_down)
        x1, x2, g1, g2 = (o.reshape(seqs, rows, width) for o in outs[:4])
        return (x1, x2, g1, g2, outs[4].reshape(w_qkv.shape), outs[5].reshape(w_out.shape), outs[6], outs[7])

    return jax.shard_map(local_backward, mesh=mesh, in_specs=(act_spec, act_spec, act_spec, act_spec) + weight_specs, out_specs=(act_spec, act_spec, act_spec, act_spec) + grad_specs, check_vma=False)
```

time: 450 us -> 458 us (1.018)
  Pallas kernels: 419 us -> 427 us
    pallas_call x1, Pallas kernels: 419 us -> 427 us  [local_backward(): pl.pallas_call(functools.partial(kernel, groups), out_shape=(act, act, ac...]
where the time goes in v4:
time: 458 us
  Pallas kernels  427 us (93%)
  local copies, waits for them, and re-layouts  30.1 us (7%)
    pallas_call x1, Pallas kernels, local_backward(): pl.pallas_call(functools.partial(kernel, groups), out_shape=(act, act, ac...  427 us
    unnamed x28, local copies, waits for them, and re-layouts  30.1 us

profile of v4, /device:TPU:81, one launch (start us, length us, event | category | flops | bytes accessed | tf_op | source)
XLA Modules:
  0.0 457.9 jit_solution(1422544174096945264)
XLA Ops:
  0.6 427.0 %shard_map.143 = (f32[1024,1024]{1,0:T(8,128)}, f32[1024,1024]{1,0:T(8,128)}, f32[1024,1024]{1,0:T(8,128)}, f32[1024,1024]{1,0:T(8,128)}, f32[12288,128]{1,0:T(8...) custom-call(f32[8,128,1024]{2,1,0:T(8,128)} %y1_hbm.1, ...), custom_call_target="tpu_custom_call" | custom-call | tf_op jit(solution)/shard_map/pallas_call | solution.py:700
  427.7 0.0 copy-start.2
  427.7 4.9 %copy.28 = f32[8,128,1024]{2,1,0:T(8,128)} copy(f32[8,128,1024]{2,1,0:T(8,128)} %bitcast.22) | data formatting | bytes 8388608
  432.6 0.0 copy-done.2
  432.6 0.0 copy-start.1
  432.6 0.0 slice-start.4
  432.6 2.1 copy.29
  434.8 1.6 copy-done.1
  436.3 0.0 copy-start
  436.3 0.0 slice-start.5
  436.3 2.1 copy.30
  438.5 1.8 copy-done
  440.3 0.0 slice-start.2
  440.3 2.1 copy.31
  442.4 0.0 slice-done.4
  442.4 0.0 slice-done.5
  442.4 0.0 copy-start.3
  442.4 0.0 slice-start.3
  442.5 3.2 copy.32
  445.7 1.2 copy-done.3
  446.9 0.0 slice-start
  446.9 1.3 copy.33
  448.2 0.0 slice-done.2
  448.2 0.5 slice-done.3
  448.8 0.0 slice-start.1
  448.8 4.3 copy.34
  453.0 0.0 slice-done
  453.0 1.4 slice-done.1
  454.5 3.4 copy.35
  (3 shorter events, 0.0 us)
Async XLA Ops:
  427.7 5.0 %copy-start.2 = (f32[1024,1024]{1,0:T(8,128)S(1)}, f32[1024,1024]{1,0:T(8,128)}, u32[]{:S(2)}) copy-start(f32[1024,1024]{1,0:T(8,128)} %get-tuple-element.17) | copy-start | bytes 12582916
  432.6 3.7 copy-start.1
  432.6 9.8 %slice-start.4 = ((s8[6291456]{0:T(1024)(128)(4,1)}), s8[4194304]{0:T(1024)(128)(4,1)S(1)}, s32[]{:S(2)}) async-start(s8[6291456]{0:T(1024)(128)(4,1)} %bitcast.16), calls=%async_computation.4 | async-start | bytes 8388608
  436.3 4.0 copy-start
  436.3 6.1 %slice-start.5 = ((s8[6291456]{0:T(1024)(128)(4,1)}), s8[2097152]{0:T(1024)(128)(4,1)S(1)}, s32[]{:S(2)}) async-start(s8[6291456]{0:T(1024)(128)(4,1)} %bitcast.16), calls=%async_computation.5 | async-start | bytes 4194304
  440.3 7.9 %slice-start.2 = ((s8[8388608]{0:T(1024)(128)(4,1)}), s8[4194304]{0:T(1024)(128)(4,1)S(1)}, s32[]{:S(2)}) async-start(s8[8388608]{0:T(1024)(128)(4,1)} %bitcast.14), calls=%async_computation.2 | async-start | bytes 8388608
  442.4 4.4 copy-start.3
  442.4 6.3 %slice-start.3 = ((s8[8388608]{0:T(1024)(128)(4,1)}), s8[4194304]{0:T(1024)(128)(4,1)S(1)}, s32[]{:S(2)}) async-start(s8[8388608]{0:T(1024)(128)(4,1)} %bitcast.14), calls=%async_computation.3 | async-start | bytes 8388608
  446.9 6.1 %slice-start = ((s8[8388608]{0:T(1024)(128)(4,1)}), s8[4194304]{0:T(1024)(128)(4,1)S(1)}, s32[]{:S(2)}) async-start(s8[8388608]{0:T(1024)(128)(4,1)} %bitcast.12), calls=%async_computation | async-start | bytes 8388608
  448.8 5.7 %slice-start.1 = ((s8[8388608]{0:T(1024)(128)(4,1)}), s8[4194304]{0:T(1024)(128)(4,1)S(1)}, s32[]{:S(2)}) async-start(s8[8388608]{0:T(1024)(128)(4,1)} %bitcast.12), calls=%async_computation.1 | async-start | bytes 8388608

commit v5 on v4

--- a/solution.py
+++ b/solution.py
@@ -11,6 +11,7 @@
 F32, BF16 = jnp.float32, jnp.bfloat16
 GELU_C = math.sqrt(2.0 / math.pi)
 GELU_A = 0.044715
+CHUNK = 64
 NCHIP = 4
 
 
@@ -179,8 +180,8 @@
                 cp.wait_recv()
 
         def total(self, r):
-            at = pl.ds(pl.multiple_of(k * rows + r * 16, 16), 16)
-            loc = pl.ds(pl.multiple_of(r * 16, 16), 16)
+            at = pl.ds(pl.multiple_of(k * rows + r * CHUNK, CHUNK), CHUNK)
+            loc = pl.ds(pl.multiple_of(r * CHUNK, CHUNK), CHUNK)
             return (self.part[c, at].astype(F32) + self.from_sib[c, loc].astype(F32)
                     + self.fin[loc].astype(F32) + self.dir[loc].astype(F32))
 
@@ -328,32 +329,31 @@
         PB[chip] = mm_t(grad_hid, Wu[par]).astype(BF16)
 
     def attn_fwd(chip, par):
-        QKV[chip] = mm(N2[par, chip], Wqkv[par]).astype(BF16)
+        qkv = mm(N2[par, chip], Wqkv[par]).astype(BF16)
+        QKV[chip] = qkv
+        parts = [[qkv[s * rows:(s + 1) * rows, j * head:(j + 1) * head] for j in range(3)] for s in range(2)]
+        scores = [mm_t(q, kk) * scale for q, kk, _ in parts]
+        exps = [jnp.exp(sc - jnp.max(sc, axis=-1, keepdims=True)) for sc in scores]
+        probs = [e / jnp.sum(e, axis=-1, keepdims=True) for e in exps]
         for s in range(2):
-            at = slice(s * rows, (s + 1) * rows)
-            q = QKV[chip, at, 0:head]
-            kk = QKV[chip, at, head:2 * head]
-            v = QKV[chip, at, 2 * head:3 * head]
-            sc = mm_t(q, kk) * scale
-            e = jnp.exp(sc - jnp.max(sc, axis=-1, keepdims=True))
-            prob = e / jnp.sum(e, axis=-1, keepdims=True)
-            PROB[chip, at] = prob
-            OG[chip, at, heads_of(c, k)] = mm(prob.astype(BF16), v).astype(BF16)
+            PROB[chip, s * rows:(s + 1) * rows] = probs[s]
+        outs = [mm(probs[s].astype(BF16), parts[s][2]).astype(BF16) for s in range(2)]
+        for s in range(2):
+            OG[chip, s * rows:(s + 1) * rows, heads_of(c, k)] = outs[s]
 
     def attn_bwd(chip, par):
-        grad_o2 = mm_t(D1[chip], Wo[par]).astype(BF16)
+        go = mm_t(D1[chip], Wo[par]).astype(BF16)
+        grad_o = [go[s * rows:(s + 1) * rows] for s in range(2)]
+        parts = [[QKV[chip, s * rows:(s + 1) * rows, j * head:(j + 1) * head] for j in range(3)] for s in range(2)]
+        probs = [PROB[chip, s * rows:(s + 1) * rows] for s in range(2)]
+        grad_p = [mm_t(grad_o[s], parts[s][2]) for s in range(2)]
+        dots = [jnp.sum(grad_p[s] * probs[s], axis=-1, keepdims=True) for s in range(2)]
+        grad_s = [(probs[s] * (grad_p[s] - dots[s]) * scale).astype(BF16) for s in range(2)]
+        grads = [[mm(grad_s[s], parts[s][1]), tmm(grad_s[s], parts[s][0]), tmm(probs[s].astype(BF16), grad_o[s])]
+                 for s in range(2)]
         for s in range(2):
-            at = slice(s * rows, (s + 1) * rows)
-            grad_o = grad_o2[at]
-            q = QKV[chip, at, 0:head]
-            kk = QKV[chip, at, head:2 * head]
-            v = QKV[chip, at, 2 * head:3 * head]
-            prob = PROB[chip, at]
-            grad_p = mm_t(grad_o, v)
-            grad_s = (prob * (grad_p - jnp.sum(grad_p * prob, axis=-1, keepdims=True)) * scale).astype(BF16)
-            GQ[chip, at, 0:head] = mm(grad_s, kk).astype(BF16)
-            GQ[chip, at, head:2 * head] = tmm(grad_s, q).astype(BF16)
-            GQ[chip, at, 2 * head:3 * head] = tmm(prob.astype(BF16), grad_o).astype(BF16)
+            for j in range(3):
+                GQ[chip, s * rows:(s + 1) * rows, j * head:(j + 1) * head] = grads[s][j].astype(BF16)
         PB[chip] = mm_t(GQ[chip], Wqkv[par]).astype(BF16)
 
     def flat(x):
@@ -385,9 +385,10 @@
 
     def own_rows(step):
         def body(r, _):
-            step(r, pl.ds(pl.multiple_of(r * 16, 16), 16), pl.ds(pl.multiple_of(k * rows + r * 16, 16), 16))
-            return 0
-        lax.fori_loop(0, rows // 16, body, 0)
+            step(r, pl.ds(pl.multiple_of(r * CHUNK, CHUNK), CHUNK),
+                 pl.ds(pl.multiple_of(k * rows + r * CHUNK, CHUNK), CHUNK))
+            return 0
+        lax.fori_loop(0, rows // CHUNK, body, 0)
 
     def inv_rms(x):
         return lax.rsqrt(jnp.mean(x * x, axis=-1, keepdims=True) + NORM_EPS)
@@ -428,9 +429,9 @@
 
     def chip_rows(step):
         def body(i, _):
-            step(pl.ds(pl.multiple_of(i * 16, 16), 16))
-            return 0
-        lax.fori_loop(0, 2 * rows // 16, body, 0)
+            step(pl.ds(pl.multiple_of(i * CHUNK, CHUNK), CHUNK))
+            return 0
+        lax.fori_loop(0, 2 * rows // CHUNK, body, 0)
 
     def attn_apply(chip, par):
         q = 1 - par

time: 458 us -> 404 us (0.88)
  Pallas kernels: 427 us -> 373 us
    pallas_call x1, Pallas kernels: 427 us -> 373 us  [local_backward(): pl.pallas_call(functools.partial(kernel, groups), out_shape=(act, act, ac...]
where the time goes in v5:
time: 404 us
  Pallas kernels  373 us (92%)
  local copies, waits for them, and re-layouts  30.1 us (7%)
    pallas_call x1, Pallas kernels, local_backward(): pl.pallas_call(functools.partial(kernel, groups), out_shape=(act, act, ac...  373 us
    unnamed x28, local copies, waits for them, and re-layouts  30.1 us

profile of v5, /device:TPU:81, one launch (start us, length us, event | category | flops | bytes accessed | tf_op | source)
XLA Modules:
  0.0 403.9 jit_solution(9642705643866004285)
XLA Ops:
  0.6 373.1 %shard_map.143 = (f32[1024,1024]{1,0:T(8,128)}, f32[1024,1024]{1,0:T(8,128)}, f32[1024,1024]{1,0:T(8,128)}, f32[1024,1024]{1,0:T(8,128)}, f32[12288,128]{1,0:T(8...) custom-call(f32[8,128,1024]{2,1,0:T(8,128)} %y1_hbm.1, ...), custom_call_target="tpu_custom_call" | custom-call | tf_op jit(solution)/shard_map/pallas_call | solution.py:701
  373.7 0.0 copy-start.2
  373.7 4.9 %copy.28 = f32[8,128,1024]{2,1,0:T(8,128)} copy(f32[8,128,1024]{2,1,0:T(8,128)} %bitcast.22) | data formatting | bytes 8388608
  378.7 0.0 copy-done.2
  378.7 0.0 copy-start.1
  378.7 0.0 slice-start.4
  378.7 2.1 copy.29
  380.8 1.6 copy-done.1
  382.4 0.0 copy-start
  382.4 0.0 slice-start.5
  382.4 2.1 copy.30
  384.5 1.8 copy-done
  386.3 0.0 slice-start.2
  386.3 2.1 copy.31
  388.5 0.0 slice-done.4
  388.5 0.0 slice-done.5
  388.5 0.0 copy-start.3
  388.5 0.0 slice-start.3
  388.5 3.2 copy.32
  391.7 1.2 copy-done.3
  392.9 0.0 slice-start
  392.9 1.3 copy.33
  394.2 0.0 slice-done.2
  394.2 0.5 slice-done.3
  394.8 0.0 slice-start.1
  394.8 4.3 %copy.34 = f32[4,1024,512]{2,1,0:T(8,128)} copy(f32[4,1024,512]{2,1,0:T(8,128)S(1)} %bitcast.15) | data formatting | bytes 16777216
  399.0 0.0 slice-done
  399.0 1.4 slice-done.1
  400.5 3.4 copy.35
  (3 shorter events, 0.0 us)
Async XLA Ops:
  373.7 5.0 %copy-start.2 = (f32[1024,1024]{1,0:T(8,128)S(1)}, f32[1024,1024]{1,0:T(8,128)}, u32[]{:S(2)}) copy-start(f32[1024,1024]{1,0:T(8,128)} %get-tuple-element.17) | copy-start | bytes 12582916
  378.7 3.7 copy-start.1
  378.7 9.8 %slice-start.4 = ((s8[6291456]{0:T(1024)(128)(4,1)}), s8[4194304]{0:T(1024)(128)(4,1)S(1)}, s32[]{:S(2)}) async-start(s8[6291456]{0:T(1024)(128)(4,1)} %bitcast.16), calls=%async_computation.4 | async-start | bytes 8388608
  382.4 4.0 copy-start
  382.4 6.1 %slice-start.5 = ((s8[6291456]{0:T(1024)(128)(4,1)}), s8[2097152]{0:T(1024)(128)(4,1)S(1)}, s32[]{:S(2)}) async-start(s8[6291456]{0:T(1024)(128)(4,1)} %bitcast.16), calls=%async_computation.5 | async-start | bytes 4194304
  386.3 7.9 %slice-start.2 = ((s8[8388608]{0:T(1024)(128)(4,1)}), s8[4194304]{0:T(1024)(128)(4,1)S(1)}, s32[]{:S(2)}) async-start(s8[8388608]{0:T(1024)(128)(4,1)} %bitcast.14), calls=%async_computation.2 | async-start | bytes 8388608
  388.5 4.4 %copy-start.3 = (f32[4,128,1024]{2,1,0:T(8,128)S(1)}, f32[4,128,1024]{2,1,0:T(8,128)}, u32[]{:S(2)}) copy-start(f32[4,128,1024]{2,1,0:T(8,128)} %get-tuple-element.21) | copy-start | bytes 6291460
  388.5 6.3 %slice-start.3 = ((s8[8388608]{0:T(1024)(128)(4,1)}), s8[4194304]{0:T(1024)(128)(4,1)S(1)}, s32[]{:S(2)}) async-start(s8[8388608]{0:T(1024)(128)(4,1)} %bitcast.14), calls=%async_computation.3 | async-start | bytes 8388608
  392.9 6.1 %slice-start = ((s8[8388608]{0:T(1024)(128)(4,1)}), s8[4194304]{0:T(1024)(128)(4,1)S(1)}, s32[]{:S(2)}) async-start(s8[8388608]{0:T(1024)(128)(4,1)} %bitcast.12), calls=%async_computation | async-start | bytes 8388608
  394.8 5.7 %slice-start.1 = ((s8[8388608]{0:T(1024)(128)(4,1)}), s8[4194304]{0:T(1024)(128)(4,1)S(1)}, s32[]{:S(2)}) async-start(s8[8388608]{0:T(1024)(128)(4,1)} %bitcast.12), calls=%async_computation.1 | async-start | bytes 8388608

commit v6 on v5

--- a/solution.py
+++ b/solution.py
@@ -161,11 +161,17 @@
             for cp in self.opp:
                 cp.start()
 
-        def send_direct(self):
+        def send_left(self):
             self.add(cl)
             self.direct[0].start()
+
+        def send_right(self):
             self.add(cr)
             self.direct[1].start()
+
+        def send_direct(self):
+            self.send_left()
+            self.send_right()
 
         def send_relay(self):
             for h, (chip, cp) in enumerate(((cl, self.relay[0]), (cr, self.relay[1]))):
@@ -231,9 +237,10 @@
                       pl.ds(pl.multiple_of((grp // n) * lanes, lanes), lanes)],
             VG.at[me, pl.ds(layer * piece, piece)], wl_sem.at[layer])]
 
-    def vg_view(chip, core, h):
-        n = layers * piece // 2
-        return VG.at[2 * chip + core, pl.ds(h * n, n)]
+    def gather_pieces(i, first, n):
+        size = n * piece // 2
+        return Gather(lambda chip, core, h: VG.at[2 * chip + core, pl.ds(first * piece + h * size, size)],
+                      wg_send.at[i], wg_recv.at[i])
 
     def piece_send(layer, d):
         return pltpu.make_async_remote_copy(
@@ -245,11 +252,11 @@
         return pltpu.make_async_copy(VG.at[:, pl.ds(layer * piece, piece)], wof_hbm.at[layer, grp],
                                      wx_send.at[layer, 0])
 
-    def pieces_out():
-        for layer in reversed(range(layers)):
+    def pieces_out(which):
+        for layer in which:
             piece_keep(layer).start()
 
-            def one(d, _):
+            def one(d, _, layer=layer):
                 piece_send(layer, d).start()
                 return 0
             lax.fori_loop(1, groups, one, 0)
@@ -460,13 +467,16 @@
         elif cond is not False:
             pl.when(cond)(fn)
 
-    def partials(rs, compute, extra=()):
+    def partials(rs, stages, extra):
         def body(j, _):
             chip = order(j)
-            compute(chip)
-            rs.pair(chip).start()
-            for at, fn in extra:
-                pl.when(j == at)(fn)
+            for i, compute in enumerate(stages):
+                compute(chip)
+                if i == len(stages) - 1:
+                    rs.pair(chip).start()
+                for step, stage, fn in extra:
+                    if stage == i:
+                        pl.when(j == step)(fn)
             return 0
         lax.fori_loop(0, NCHIP, body, 0)
 
@@ -474,15 +484,15 @@
         q = 1 - par
         ag_d = gather_rows(D2, 1)
         ag_o = gather_o()
+        ag_n = gather_rows(N2.at[par], 0)
+        finish_state(rs_f, Y2.at[q], Y2.at[par], N2.at[par])
+        ag_n.start()
+        first = False if last else jnp.logical_not(not_first)
+        ag_w = None if last else gather_pieces(1, 0, layers - 1)
         if last:
-            ag_n = gather_out(x2_out, 0, Y2.at[par])
-            finish_state(rs_f, Y2.at[q], Y2.at[par], None)
-            ag_n.start()
             keep_out(x2_out, 0, Y2.at[par]).start()
         else:
-            ag_n = gather_rows(N2.at[par], 0)
-            finish_state(rs_f, Y2.at[q], Y2.at[par], N2.at[par])
-            ag_n.start()
+            when(first, ag_w.start)
             for cp in weight_copies(layer - 1, q):
                 cp.start()
         when(not_first, rs_b.send_relay)
@@ -495,19 +505,8 @@
         when(not_first, d_start)
         ag_n.far()
         ag_n.finish()
-        if last:
-            keep_out(x2_out, 0, Y2.at[par]).wait()
-            loads = [pltpu.make_async_copy(x2_out.at[pl.ds(chip * 2 * rows, 2 * rows)], PF.at[chip],
-                                           io_sem.at[0, chip, 0]) for chip in range(NCHIP)]
-            for cp in loads:
-                cp.start()
-            for chip in range(NCHIP):
-                loads[chip].wait()
-
-                def step(at):
-                    x = PF[chip, at]
-                    N2[par, chip, at] = (x * inv_rms(x)).astype(BF16)
-                chip_rows(step)
+        if not last:
+            when(first, ag_w.near)
         pieces_in(layer)
         for cp in wov_copies(layer):
             cp.start()
@@ -522,14 +521,22 @@
             return 0
         lax.fori_loop(0, NCHIP, fwd, 0)
         ag_o.start_half(1)
+
+        def rest_out():
+            ag_w.far()
+            ag_w.finish()
+            pieces_out(range(layers - 2, -1, -1))
+        if not last:
+            when(first, rest_out)
         ag_o.near0()
 
         def d_end():
             ag_d.far()
             ag_d.finish()
         when(not_first, d_end)
-        partials(rs_b, lambda chip: mlp_bwd(chip, par), ((0, ag_o.near1), (1, rs_b.send_opp)))
-        rs_b.send_direct()
+        partials(rs_b, (lambda chip: mlp_bwd(chip, par),),
+                 ((0, 0, ag_o.near1), (1, 0, rs_b.send_opp), (2, 0, rs_b.send_left)))
+        rs_b.send_right()
         for cp in wov_copies(layer):
             cp.wait()
         ag_o.far()
@@ -541,10 +548,8 @@
         for cp in weight_copies(layer - 1, q):
             cp.wait()
 
-        def fwd(chip):
-            attn_apply(chip, par)
-            mlp_fwd(chip, q)
-        partials(rs_f, fwd, ((0, rs_b.send_relay), (1, rs_f.send_opp)))
+        partials(rs_f, (lambda chip: attn_apply(chip, par), lambda chip: mlp_fwd(chip, q)),
+                 ((0, 1, rs_b.send_relay), (1, 1, rs_f.send_opp)))
         finish_sum(rs_b, D1)
         ag_d.start()
         rs_f.send_direct()
@@ -556,11 +561,8 @@
         attn_back(par)
 
     def attn_back(par):
-        def bwd(chip):
-            cot_apply(chip, par)
-            attn_bwd(chip, par)
-        partials(rs_b, bwd, ((1, rs_b.send_opp),))
-        rs_b.send_direct()
+        partials(rs_b, (lambda chip: cot_apply(chip, par), lambda chip: attn_bwd(chip, par)),
+                 ((1, 0, rs_b.send_opp), (2, 1, rs_b.send_left), (3, 0, rs_b.send_right)))
 
     top = layers - 1
     tp = top % 2
@@ -607,19 +609,19 @@
 
     each_pair(lambda chip, s: load_rows(y1_hbm, Y1.at[tp], 0, chip, s).start())
     each_pair(lambda chip, s: load_rows(c2_hbm, C1, 1, chip, s).start())
-    ag_w = Gather(vg_view, wg_send, wg_recv)
+    ag_w = gather_pieces(0, top, 1)
     for layer in range(layers):
         for cp in own_piece_copies(layer):
             cp.wait()
     ag_w.start()
     for cp in weight_copies(top, tp):
         cp.wait()
-    partials(rs_f, top_fwd, ((1, rs_f.send_opp),))
+    partials(rs_f, (top_fwd,), ((1, 0, rs_f.send_opp),))
     ag_w.near()
     rs_f.send_direct()
     ag_w.far()
     ag_w.finish()
-    pieces_out()
+    pieces_out((top,))
     rs_f.send_relay()
     cast_c2()
     for cp in loads:
@@ -660,23 +662,29 @@
     ag_d1.start()
     lax.fori_loop(0, NCHIP, x1_rows, 0)
     ag_d1.near()
+    ag_x = gather_out(x2_out, 0, Y2.at[0])
+    ag_x.start()
     mlp_wgrad(0, 0)
     ag_d1.far()
     ag_d1.finish()
     attn_back(0)
     each_chip(lambda chip: put_g1(chip).start())
     rs_b.send_relay()
+    ag_x.near()
     attn_wgrad(0, 0)
     finish_cot(rs_b, C2, Y2.at[0], None)
     last = gather_out(g2_out, 1, C2)
     last.start()
     keep_out(g2_out, 1, C2).start()
+    ag_x.far()
     last.near()
     last.far()
     each_chip(lambda chip: put_x1(chip).wait())
     each_chip(lambda chip: put_g1(chip).wait())
     pieces_sent()
+    keep_out(x2_out, 0, Y2.at[0]).wait()
     keep_out(g2_out, 1, C2).wait()
+    ag_x.finish()
     last.finish()
 
 
@@ -742,7 +750,7 @@
                 pltpu.VMEM((seqs, head, width), BF16),
                 dma((4, 14)), dma((4, 14)), dma((2, 10)), dma((2, 10)), dma((2, 14)), dma((2, 14)),
                 dma((2, 6)), dma((4, 2)), dma((2, NCHIP, 2)), dma((2,)),
-                dma((14,)), dma((14,)), dma((layers, groups)), dma((layers, groups)),
+                dma((2, 14)), dma((2, 14)), dma((layers, groups)), dma((layers, groups)),
                 dma((max(layers * max(1, piece // head), groups, width // 128),)),
             ],
             compiler_params=pltpu.CompilerParams(collective_id=0, has_side_effects=True,

time: 404 us -> 394 us (0.975)
  Pallas kernels: 373 us -> 363 us
    pallas_call x1, Pallas kernels: 373 us -> 363 us  [local_backward(): pl.pallas_call(functools.partial(kernel, groups), out_shape=(act, act, ac...]
where the time goes in v6:
time: 394 us
  Pallas kernels  363 us (92%)
  local copies, waits for them, and re-layouts  30.1 us (8%)
    pallas_call x1, Pallas kernels, local_backward(): pl.pallas_call(functools.partial(kernel, groups), out_shape=(act, act, ac...  363 us
    unnamed x28, local copies, waits for them, and re-layouts  30.1 us

profile of v6, /device:TPU:81, one launch (start us, length us, event | category | flops | bytes accessed | tf_op | source)
XLA Modules:
  0.0 393.8 jit_solution(8563993926864439247)
XLA Ops:
  0.6 363.0 %shard_map.143 = (f32[1024,1024]{1,0:T(8,128)}, f32[1024,1024]{1,0:T(8,128)}, f32[1024,1024]{1,0:T(8,128)}, f32[1024,1024]{1,0:T(8,128)}, f32[12288,128]{1,0:T(8...) custom-call(f32[8,128,1024]{2,1,0:T(8,128)} %y1_hbm.1, ...), custom_call_target="tpu_custom_call" | custom-call | tf_op jit(solution)/shard_map/pallas_call | solution.py:709
  363.7 0.0 copy-start.2
  363.7 4.9 %copy.28 = f32[8,128,1024]{2,1,0:T(8,128)} copy(f32[8,128,1024]{2,1,0:T(8,128)} %bitcast.22) | data formatting | bytes 8388608
  368.6 0.0 copy-done.2
  368.6 0.0 copy-start.1
  368.6 0.0 slice-start.4
  368.6 2.1 copy.29
  370.7 1.6 copy-done.1
  372.3 0.0 copy-start
  372.3 0.0 slice-start.5
  372.3 2.1 copy.30
  374.4 1.8 copy-done
  376.3 0.0 slice-start.2
  376.3 2.1 copy.31
  378.4 0.0 slice-done.4
  378.4 0.0 slice-done.5
  378.4 0.0 copy-start.3
  378.4 0.0 slice-start.3
  378.4 3.2 copy.32
  381.6 1.2 copy-done.3
  382.9 0.0 slice-start
  382.9 1.3 copy.33
  384.2 0.0 slice-done.2
  384.2 0.5 slice-done.3
  384.7 0.0 slice-start.1
  384.7 4.3 %copy.34 = f32[4,1024,512]{2,1,0:T(8,128)} copy(f32[4,1024,512]{2,1,0:T(8,128)S(1)} %bitcast.15) | data formatting | bytes 16777216
  389.0 0.0 slice-done
  389.0 1.4 slice-done.1
  390.4 3.4 copy.35
  (3 shorter events, 0.0 us)
Async XLA Ops:
  363.7 5.0 %copy-start.2 = (f32[1024,1024]{1,0:T(8,128)S(1)}, f32[1024,1024]{1,0:T(8,128)}, u32[]{:S(2)}) copy-start(f32[1024,1024]{1,0:T(8,128)} %get-tuple-element.17) | copy-start | bytes 12582916
  368.6 3.7 copy-start.1
  368.6 9.8 %slice-start.4 = ((s8[6291456]{0:T(1024)(128)(4,1)}), s8[4194304]{0:T(1024)(128)(4,1)S(1)}, s32[]{:S(2)}) async-start(s8[6291456]{0:T(1024)(128)(4,1)} %bitcast.16), calls=%async_computation.4 | async-start | bytes 8388608
  372.3 4.0 %copy-start = (f32[1024,1024]{1,0:T(8,128)S(1)}, f32[1024,1024]{1,0:T(8,128)}, u32[]{:S(2)}) copy-start(f32[1024,1024]{1,0:T(8,128)} %get-tuple-element.19) | copy-start | bytes 12582916
  372.3 6.1 %slice-start.5 = ((s8[6291456]{0:T(1024)(128)(4,1)}), s8[2097152]{0:T(1024)(128)(4,1)S(1)}, s32[]{:S(2)}) async-start(s8[6291456]{0:T(1024)(128)(4,1)} %bitcast.16), calls=%async_computation.5 | async-start | bytes 4194304
  376.3 7.9 %slice-start.2 = ((s8[8388608]{0:T(1024)(128)(4,1)}), s8[4194304]{0:T(1024)(128)(4,1)S(1)}, s32[]{:S(2)}) async-start(s8[8388608]{0:T(1024)(128)(4,1)} %bitcast.14), calls=%async_computation.2 | async-start | bytes 8388608
  378.4 4.4 %copy-start.3 = (f32[4,128,1024]{2,1,0:T(8,128)S(1)}, f32[4,128,1024]{2,1,0:T(8,128)}, u32[]{:S(2)}) copy-start(f32[4,128,1024]{2,1,0:T(8,128)} %get-tuple-element.21) | copy-start | bytes 6291460
  378.4 6.3 %slice-start.3 = ((s8[8388608]{0:T(1024)(128)(4,1)}), s8[4194304]{0:T(1024)(128)(4,1)S(1)}, s32[]{:S(2)}) async-start(s8[8388608]{0:T(1024)(128)(4,1)} %bitcast.14), calls=%async_computation.3 | async-start | bytes 8388608
  382.9 6.1 %slice-start = ((s8[8388608]{0:T(1024)(128)(4,1)}), s8[4194304]{0:T(1024)(128)(4,1)S(1)}, s32[]{:S(2)}) async-start(s8[8388608]{0:T(1024)(128)(4,1)} %bitcast.12), calls=%async_computation | async-start | bytes 8388608
  384.7 5.7 %slice-start.1 = ((s8[8388608]{0:T(1024)(128)(4,1)}), s8[4194304]{0:T(1024)(128)(4,1)S(1)}, s32[]{:S(2)}) async-start(s8[8388608]{0:T(1024)(128)(4,1)} %bitcast.12), calls=%async_computation.1 | async-start | bytes 8388608

commit v7 on v6

--- a/solution.py
+++ b/solution.py
@@ -686,6 +686,45 @@
     keep_out(g2_out, 1, C2).wait()
     ag_x.finish()
     last.finish()
+
+
+PARTS = 8
+
+
+def copy_kernel(*refs):
+    n = (len(refs) - 2) // 3
+    ins, outs, bufs, rsem, wsem = refs[:n], refs[n:2 * n], refs[2 * n:3 * n], refs[-2], refs[-1]
+
+    def part(ref, p):
+        if len(ref.shape) == 2:
+            size = ref.shape[0] // PARTS
+            return ref.at[pl.ds(p * size, size)]
+        per = PARTS // ref.shape[0]
+        size = ref.shape[1] // per
+        return ref.at[p // per, pl.ds((p % per) * size, size)]
+    todo = [(i, p) for i in range(n) for p in range(PARTS)]
+    reads = [pltpu.make_async_copy(part(ins[i], p), part(bufs[i], p), rsem.at[i, p]) for i, p in todo]
+    writes = [pltpu.make_async_copy(part(bufs[i], p), part(outs[i], p), wsem.at[i, p]) for i, p in todo]
+    for cp in reads:
+        cp.start()
+    for rd, wr in zip(reads, writes):
+        rd.wait()
+        wr.start()
+    for cp in writes:
+        cp.wait()
+
+
+def copy_out(arrays):
+    shapes = [jax.ShapeDtypeStruct(a.shape, a.dtype) for a in arrays]
+    sems = pltpu.SemaphoreType.DMA((len(arrays), PARTS))
+    return pl.pallas_call(
+        copy_kernel,
+        out_shape=shapes,
+        in_specs=[pl.BlockSpec(memory_space=pl.ANY)] * len(arrays),
+        out_specs=[pl.BlockSpec(memory_space=pl.ANY)] * len(arrays),
+        scratch_shapes=[pltpu.VMEM(a.shape, a.dtype) for a in arrays] + [sems, sems],
+        compiler_params=pltpu.CompilerParams(vmem_limit_bytes=67043328),
+    )(*arrays)
 
 
 def solution(mesh):
@@ -756,6 +795,7 @@
             compiler_params=pltpu.CompilerParams(collective_id=0, has_side_effects=True,
                                                  vmem_limit_bytes=67043328),
         )(out_y1, out_y2, cot_y1, cot_y2, wq, wo, w_up, w_down)
+        outs = copy_out(outs[:8])
         x1, x2, g1, g2 = (o.reshape(seqs, rows, width) for o in outs[:4])
         return (x1, x2, g1, g2, outs[4].reshape(w_qkv.shape), outs[5].reshape(w_out.shape), outs[6], outs[7])
 

time: 394 us -> 393 us (level)
  local copies, waits for them, and re-layouts: 30.1 us -> 0 us
  Pallas kernels: 363 us -> 392 us
    unnamed x28 -> x0, local copies, waits for them, and re-layouts: 30.1 us -> none
    pallas_call x0 -> x1, Pallas kernels: none -> 28.5 us  [copy_out(): pl.pallas_call(copy_kernel, out_shape=shapes, in_specs=[pl.BlockSpec(memo...]
where the time goes in v7:
time: 393 us; the launch traced here: 392 us
  Pallas kernels  392 us (100%)
    pallas_call x1, Pallas kernels, local_backward(): pl.pallas_call(functools.partial(kernel, groups), out_shape=(act, act, ac...  363 us
    pallas_call x1, Pallas kernels, copy_out(): pl.pallas_call(copy_kernel, out_shape=shapes, in_specs=[pl.BlockSpec(memo...  28.5 us

profile of v7, /device:TPU:81, one launch (start us, length us, event | category | flops | bytes accessed | tf_op | source)
XLA Modules:
  0.0 392.3 jit_solution(2089423002483043254)
XLA Ops:
  0.6 363.0 %shard_map.143 = (f32[1024,1024]{1,0:T(8,128)}, f32[1024,1024]{1,0:T(8,128)}, f32[1024,1024]{1,0:T(8,128)}, f32[1024,1024]{1,0:T(8,128)}, f32[12288,128]{1,0:T(8...) custom-call(f32[8,128,1024]{2,1,0:T(8,128)} %y1_hbm.1, ...), custom_call_target="tpu_custom_call" | custom-call | tf_op jit(solution)/shard_map/pallas_call | solution.py:748
  363.7 28.5 %shard_map.144 = (f32[1024,1024]{1,0:T(8,128)}, f32[1024,1024]{1,0:T(8,128)}, f32[1024,1024]{1,0:T(8,128)}, f32[1024,1024]{1,0:T(8,128)}, f32[12288,128]{1,0:T(8...) custom-call(f32[1024,1024]{1,0:T(8,128)} %get-tuple-element.24.refs_0_, ...), custom_call_target="tpu_custom_call" | custom-call | tf_op jit(solution)/shard_map/pallas_call | solution.py:720

commit v8 on v7

--- a/solution.py
+++ b/solution.py
@@ -11,7 +11,7 @@
 F32, BF16 = jnp.float32, jnp.bfloat16
 GELU_C = math.sqrt(2.0 / math.pi)
 GELU_A = 0.044715
-CHUNK = 64
+CHUNK = 128
 NCHIP = 4
 
 

time: 393 us -> 388 us (0.987)
  Pallas kernels: 392 us -> 387 us
    pallas_call x1, Pallas kernels: 363 us -> 359 us  [local_backward(): pl.pallas_call(functools.partial(kernel, groups), out_shape=(act, act, ac...]
where the time goes in v8:
time: 388 us
  Pallas kernels  387 us (100%)
    pallas_call x1, Pallas kernels, local_backward(): pl.pallas_call(functools.partial(kernel, groups), out_shape=(act, act, ac...  359 us
    pallas_call x1, Pallas kernels, copy_out(): pl.pallas_call(copy_kernel, out_shape=shapes, in_specs=[pl.BlockSpec(memo...  28.5 us

profile of v8, /device:TPU:81, one launch (start us, length us, event | category | flops | bytes accessed | tf_op | source)
XLA Modules:
  0.0 388.0 jit_solution(15728050235392169023)
XLA Ops:
  0.6 358.7 %shard_map.143 = (f32[1024,1024]{1,0:T(8,128)}, f32[1024,1024]{1,0:T(8,128)}, f32[1024,1024]{1,0:T(8,128)}, f32[1024,1024]{1,0:T(8,128)}, f32[12288,128]{1,0:T(8...) custom-call(f32[8,128,1024]{2,1,0:T(8,128)} %y1_hbm.1, ...), custom_call_target="tpu_custom_call" | custom-call | tf_op jit(solution)/shard_map/pallas_call | solution.py:748
  359.4 28.5 %shard_map.144 = (f32[1024,1024]{1,0:T(8,128)}, f32[1024,1024]{1,0:T(8,128)}, f32[1024,1024]{1,0:T(8,128)}, f32[1024,1024]{1,0:T(8,128)}, f32[12288,128]{1,0:T(8...) custom-call(f32[1024,1024]{1,0:T(8,128)} %get-tuple-element.24.refs_0_, ...), custom_call_target="tpu_custom_call" | custom-call | tf_op jit(solution)/shard_map/pallas_call | solution.py:720
